TPU v7x, 512 devices: a whole 4x4x16 slice. The times are simulated.
512 devices in a mesh: vocab: 32 (over x, z_lo, core), batch: 16 (over y, z_hi).
Axes of the slice: x: 4, y: 4, z: 16 (z_hi: 4, z_lo: 4; z = z_hi * 4 + z_lo), core: 2. Of those that a mesh axis runs over, the one named last changes fastest.
Arguments:
- neighbour_ids: int32 [512, 128], P(('vocab', 'batch')), may hold values from 0 to 127999, as said below
- query_states: bfloat16 [256, 64, 4096], P('vocab', None, 'batch'), may hold values from -6 to 6
- table: bfloat16 [128000, 4096], P('vocab', 'batch'), may hold values from -6 to 6
- in_proj: bfloat16 [4096, 896], P('batch'), may hold values from -0.09375 to 0.09375
- kv_proj: bfloat16 [4096, 896], P('batch'), may hold values from -0.09375 to 0.09375
- norm_self: float32 [896], replicated, may hold values from 0.25 to 1.75
- self_qkv: bfloat16 [896, 1344], P('batch'), may hold values from -0.1875 to 0.1875
- self_out: bfloat16 [448, 896], P('batch'), may hold values from -0.25 to 0.25
- norm_cross: float32 [896], replicated, may hold values from 0.25 to 1.75
- cross_q: bfloat16 [896, 448], P('batch'), may hold values from -0.1875 to 0.1875
- cross_out: bfloat16 [448, 896], P('batch'), may hold values from -0.25 to 0.25
Outputs:
- encoded: bfloat16 [512, 128, 896], P(('vocab', 'batch'))
Inputs may be any that keep to these rules, and one draw needn't show every extreme that they name: `neighbour_ids`: ids fall in 32 consecutive blocks of 4000 ids; of one device's 1 * 128 tokens (rows of one device), at most 4 lie in one block, and in every such group some block holds exactly 4.
All inputs are finite; a program needn't handle non-finite values.
Results may differ from a plain program's by a relative error of at most 0.019.
Values may be sent and summed in bfloat16 or wider, within the bound.
A program may use at most 64 MiB of HBM per device.

v0:
```python
import jax
import jax.numpy as jnp
from jax import lax
from jax.sharding import Mesh
from jax.sharding import PartitionSpec as P

HEAD = 64
K = 2
BATCH = ("batch_0", "batch_1")
VOCAB_BATCH = ("vocab", "batch_0", "batch_1")


def joined_along(parts, dim):
    parts = jnp.moveaxis(parts, 0, dim)
    dims = parts.shape
    return parts.reshape(*dims[:dim], dims[dim] * dims[dim + 1], *dims[dim + 2 :])


def copy_for_each(x, axis):
    copies = jnp.broadcast_to(x, (lax.axis_size(axis), *x.shape))
    return lax.all_to_all(copies, axis, split_axis=0, concat_axis=0, tiled=True)


def gathered_copies(x, axis, dim):
    return joined_along(copy_for_each(x, axis), dim)


def own_rows(terms, axes):
    total = terms.astype(jnp.bfloat16)
    for axis in axes:
        total = lax.psum_scatter(total, axis, scatter_dimension=0, tiled=True)
    return total.astype(jnp.float32)


def rows_for(lines, length):
    spare = -len(lines) % length
    return jnp.pad(lines, [(0, spare)] + [(0, 0)] * (lines.ndim - 1))


def cut_along(x, dim, length):
    dims = x.shape
    parts = x.reshape(*dims[:dim], length, dims[dim] // length, *dims[dim + 1 :])
    return jnp.moveaxis(parts, dim, 0)


def summed_on_arrival(x, axis, dim):
    parts = cut_along(x, dim, lax.axis_size(axis))
    arrived = lax.all_to_all(parts, axis, split_axis=0, concat_axis=0, tiled=True)
    return arrived.astype(jnp.float32).sum(axis=0)


def nested_sum(x, axes):
    lines = x.reshape(-1, x.shape[-1])
    padded = rows_for(lines, lax.axis_size(axes))
    whole = gathered_copies(summed_on_arrival(padded, axes, 0).astype(jnp.bfloat16), axes, 0)
    return lax.slice_in_dim(whole, 0, len(lines)).reshape(x.shape).astype(jnp.float32)


def gather_together(arrays, axis, dims):
    flat = jnp.concatenate([a.reshape(-1) for a in arrays])
    lines, at, finished = (lax.all_gather(flat, axis), 0, [])
    for a, dim in zip(arrays, dims):
        parts = lines[:, at : at + a.size].reshape(-1, *a.shape)
        finished.append(joined_along(parts, dim))
        at += a.size
    return tuple(finished)


def norm_rows(values, gain):
    scale = lax.rsqrt(jnp.mean(values * values, axis=-1, keepdims=True) + 1e-06)
    return values * scale * gain


def attend(queries, keys, values):
    scores = jnp.einsum(
        "nahd,nbhd->nhab", queries, keys, preferred_element_type=jnp.float32
    ) * HEAD ** (-0.5)
    weights = jax.nn.softmax(scores, axis=-1).astype(jnp.bfloat16)
    return jnp.einsum(
        "nhab,nbhd->nahd", weights, values, preferred_element_type=jnp.float32
    ).astype(jnp.bfloat16)


def encode(start_rows, span_kv, norm_self, self_qkv, self_out, norm_cross, cross_q, cross_out):
    count, length, width = start_rows.shape
    inner = self_out.shape[0]
    heads = inner // HEAD
    keys_len = span_kv.shape[1]
    stream = start_rows.astype(jnp.float32)
    self_in = norm_rows(stream, norm_self).astype(jnp.bfloat16)
    mixed = jnp.einsum("nrd,de->nre", self_in, self_qkv, preferred_element_type=jnp.float32).astype(
        jnp.bfloat16
    )
    queries = mixed[:, :, :inner].reshape(count, length, heads, HEAD)
    keys = mixed[:, :, inner : 2 * inner].reshape(count, length, heads, HEAD)
    values = mixed[:, :, 2 * inner :].reshape(count, length, heads, HEAD)
    self_heads = attend(queries, keys, values).reshape(count, length, inner)
    stream = stream + jnp.einsum(
        "nre,ed->nrd", self_heads, self_out, preferred_element_type=jnp.float32
    )
    cross_in = norm_rows(stream, norm_cross).astype(jnp.bfloat16)
    cross_query = jnp.einsum(
        "nrd,de->nre", cross_in, cross_q, preferred_element_type=jnp.float32
    ).astype(jnp.bfloat16)
    cross_keys = span_kv[:, :, :inner].reshape(count, keys_len, heads, HEAD)
    cross_values = span_kv[:, :, inner:].reshape(count, keys_len, heads, HEAD)
    cross_heads = attend(
        cross_query.reshape(count, length, heads, HEAD), cross_keys, cross_values
    ).reshape(count, length, inner)
    stream = stream + jnp.einsum(
        "nre,ed->nrd", cross_heads, cross_out, preferred_element_type=jnp.float32
    )
    return stream.astype(jnp.bfloat16)


def body(
    neighbour_ids,
    query_states,
    table,
    in_proj,
    kv_proj,
    norm_self,
    self_qkv,
    self_out,
    norm_cross,
    cross_q,
    cross_out,
):
    shards = lax.axis_size("vocab")
    groups = lax.axis_size(BATCH)
    table_rows = table.shape[0]
    per_device, length = neighbour_ids.shape
    flat_ids = neighbour_ids.reshape(-1)
    tokens = flat_ids.shape[0]
    room = max(2, 9 * tokens // (8 * shards))
    slots = shards * room
    owner = flat_ids // table_rows
    member = (owner[:, None] == jnp.arange(shards, dtype=jnp.int32)[None, :]).astype(jnp.int32)
    before = jnp.cumsum(member, axis=0) - member
    within = jnp.sum(before * member, axis=1)
    target = owner * room + within
    placed = target[:, None] == jnp.arange(slots, dtype=jnp.int32)[None, :]
    outgoing = jnp.max(jnp.where(placed, flat_ids[:, None], -1), axis=0).reshape(shards, room)
    arrived = lax.all_to_all(outgoing, "vocab", split_axis=0, concat_axis=0, tiled=True)
    wanted = gathered_copies(arrived.reshape(1, slots), BATCH, 0)
    local_row = wanted - lax.axis_index("vocab") * table_rows
    present = wanted >= 0
    looked = jnp.take(table, jnp.clip(local_row, 0, table_rows - 1), axis=0)
    looked = jnp.where(present[:, :, None], looked, jnp.zeros_like(looked))
    selector = placed.astype(jnp.bfloat16)
    enc_width = in_proj.shape[1]
    slot_rows = own_rows(
        jnp.einsum("bsd,de->bse", looked, in_proj, preferred_element_type=jnp.float32), BATCH
    )[0].astype(jnp.bfloat16)
    returned = lax.all_to_all(
        slot_rows.reshape(shards, room, enc_width), "vocab", split_axis=0, concat_axis=0, tiled=True
    )
    start_rows = jnp.dot(
        selector, returned.reshape(slots, enc_width), preferred_element_type=jnp.float32
    ).astype(jnp.bfloat16)
    local_terms = jnp.einsum(
        "cqd,de->cqe", query_states, kv_proj, preferred_element_type=jnp.float32
    ).astype(jnp.bfloat16)
    pair_sum = nested_sum(local_terms.astype(jnp.float32).astype(jnp.bfloat16), BATCH)
    span_count = query_states.shape[0]
    neighbour_index = (
        lax.axis_index("vocab") * groups + lax.axis_index(BATCH)
    ) * per_device + jnp.arange(per_device, dtype=jnp.int32)
    span_index = neighbour_index // K - lax.axis_index("vocab") * span_count
    span_kv = jnp.take(pair_sum, span_index, axis=0).astype(jnp.bfloat16)
    qkv_whole, out_whole, query_whole, cross_whole = gather_together(
        (self_qkv, self_out, cross_q, cross_out), BATCH, (0, 0, 0, 0)
    )
    return encode(
        start_rows.reshape(per_device, length, enc_width),
        span_kv,
        norm_self,
        qkv_whole,
        out_whole,
        norm_cross,
        query_whole,
        cross_whole,
    )


def solution(mesh):
    finer = Mesh(mesh.devices.reshape(mesh.shape["vocab"], 4, 4), ("vocab", "batch_0", "batch_1"))
    in_specs = (
        P(VOCAB_BATCH, None),
        P("vocab", None, BATCH),
        P("vocab", BATCH),
        P(BATCH, None),
        P(BATCH, None),
        P(),
        P(BATCH, None),
        P(BATCH, None),
        P(),
        P(BATCH, None),
        P(BATCH, None),
    )
    out_specs = P(VOCAB_BATCH, None, None)
    return jax.shard_map(body, mesh=finer, in_specs=in_specs, out_specs=out_specs, check_vma=False)
```

profile of v0, /device:TPU:1, one launch (start us, length us, event | category | flops | bytes accessed | tf_op | source)
XLA Modules:
  0.0 347.5 jit_solution(2813093028209143513)
XLA Ops:
  7.4 0.8 and_select_fusion
  8.2 0.1 fusion.25
  8.3 0.2 reduce_window_sum.11
  8.4 0.2 select_reduce_fusion.1
  8.6 0.7 multiply_add_fusion
  9.3 0.8 select_reduce_fusion
  10.1 0.1 all_to_all.18
  10.2 17.0 %all_to_all.29 = s32[32,1,4]{2,1,0:T(1,128)S(1)} all-to-all(s32[32,1,4]{2,1,0:T(1,128)S(1)} %bitcast.86), channel_id=1, replica_groups=mesh['vocab'=32,'batch_0'=4,'batch_1'=4] {'vocab'}, dimensions={0} | all-to-all | bytes 1024 | tf_op jit(solution)/shard_map/all_to_all | solution.py:144
  27.2 0.5 broadcast.217
  27.7 0.7 reduce.16
  28.4 0.1 reshape.270
  28.5 0.6 broadcast_in_dim.66
  29.1 14.8 %all-to-all-start.1 = ((s32[16,1,128]{2,1,0:T(1,128)}), s32[16,1,128]{2,1,0:T(1,128)S(1)}, u32[]{:S(2)}, u32[]{:S(2)}) async-start(s32[16,1,128]{2,1,0:T(1,128)} %broadcast_in_dim.66), calls=%async_computation.1 | async-start | bytes 16384 | tf_op jit(solution)/shard_map/all_to_all | solution.py:21
  44.0 0.0 reduce-scatter.3.cloned.1.call-start
  44.0 13.5 %all-to-all-done.1 = s32[16,1,128]{2,1,0:T(1,128)S(1)} async-done(((s32[16,1,128]{2,1,0:T(1,128)}), s32[16,1,128]{2,1,0:T(1,128)S(1)}, u32[]{:S(2)}, u32[]{:S(2)}) %all-to-all-start.1) | async-done | bytes 8224 | tf_op jit(solution)/shard_map/all_to_all | solution.py:21
  57.6 7.5 %gather_fusion = bf16[2048,256]{1,0:T(8,128)(2,1)S(1)} fusion(bf16[4000,256]{1,0:T(8,128)(2,1)S(1)} %copy-done, s32[2048]{0:T(1024)S(1)} %fusion.28), kind=kCustom, calls=%fused_computation | custom fusion | bytes 2105344 | tf_op jit(solution)/shard_map/jit(_take)/gather | solution.py:148
  65.1 3.9 %convolution_convert_fusion = bf16[16,128,896]{2,1,0:T(8,128)(2,1)} fusion(bf16[16,128,256]{2,1,0:T(8,128)(2,1)S(1)} %bitcast.72, pred[16,128]{1,0:T(8,128)(4,1)S(1)} %compare_and_fusion, pred[16,128]{1,0:T(8,128)(4,1)S(1)} %compare_bitcast_fusion, bf16[256,896]{1,0:T(8,128)(2,1)} %param.14), kind=kOutput, calls=%fused_computation.3 | convolution fusion | flops 942407680 | bytes 5181440 | tf_op jit(solution)/shard_map/bsd,de->bse/dot_general | solution.py:153
  69.0 0.0 copy-start.2
  69.0 0.0 copy-start.3
  69.0 0.0 reduce-scatter.3.cloned.1.call-update
  69.1 0.0 all-gather.3.cloned.1.call-start
  69.1 0.8 copy-done.4
  69.9 0.2 reshape.272
  70.1 0.1 reshape.273
  70.2 0.1 reshape.274
  70.3 0.1 reshape.275
  70.4 0.8 pad_maximum_fusion
  71.2 0.0 all-gather.3.cloned.1.call-update
  71.2 0.4 convolution_convert_fusion.2
  71.7 65.1 %all_to_all.30 = bf16[16,32,896]{2,1,0:T(8,128)(2,1)S(1)} all-to-all(bf16[16,32,896]{2,1,0:T(8,128)(2,1)S(1)} %bitcast.70), channel_id=1, replica_groups=mesh['vocab'=32,'batch_0'=4,'batch_1'=4] {'batch_0','batch_1'}, dimensions={0} | all-to-all | bytes 1835008 | tf_op jit(solution)/shard_map/all_to_all | solution.py:48
  136.7 0.1 reduce_sum.60
  136.9 1.0 broadcast_in_dim.73
  137.9 14.7 %all-to-all-start.4 = ((bf16[16,32,896]{2,1,0:T(8,128)(2,1)}), bf16[16,32,896]{2,1,0:T(8,128)(2,1)S(1)}, u32[]{:S(2)}, u32[]{:S(2)}) async-start(bf16[16,32,896]{2,1,0:T(8,128)(2,1)} %broadcast_in_dim.73), calls=%async_computation.6 | async-start | bytes 1835008 | tf_op jit(solution)/shard_map/all_to_all | solution.py:21
  152.6 0.0 reduce-scatter.5.cloned.1.call-start
  152.6 0.0 reduce-scatter.3.cloned.1.call-done
  152.6 0.7 reduce-scatter.5.cloned.1.call-update
  153.3 41.5 %all-to-all-done.4 = bf16[16,32,896]{2,1,0:T(8,128)(2,1)S(1)} async-done(((bf16[16,32,896]{2,1,0:T(8,128)(2,1)}), bf16[16,32,896]{2,1,0:T(8,128)(2,1)S(1)}, u32[]{:S(2)}, u32[]{:S(2)}) %all-to-all-start.4) | async-done | bytes 917536 | tf_op jit(solution)/shard_map/all_to_all | solution.py:21
  194.8 0.1 fusion.39
  194.9 0.1 reshape.283
  195.1 0.1 copy.30
  195.2 94.8 %all-gather.3.cloned.1.call-done = bf16[2408448]{0:T(1024)(128)(2,1)} async-done(((bf16[150528]{0:T(1024)(128)(2,1)}), bf16[2408448]{0:T(1024)(128)(2,1)}) %all-gather.3.cloned.1.call-update) | async-done | bytes 4816912 | tf_op jit(solution)/shard_map/all_gather | solution.py:61
  290.0 5.2 %reshape.322 = bf16[16,150528]{1,0:T(8,128)(2,1)} reshape(bf16[2408448]{0:T(1024)(128)(2,1)} %all-gather.3.cloned.1.call-done) | data formatting | bytes 9633792 | tf_op jit(solution)/shard_map/all_gather | solution.py:61
  295.2 1.7 convert_element_type.96
  296.9 13.5 %all-to-all-start.2 = ((bf16[32,4,896]{2,1,0:T(4,128)(2,1)}), bf16[32,4,896]{2,1,0:T(4,128)(2,1)S(1)}, u32[]{:S(2)}, u32[]{:S(2)}) async-start(bf16[32,4,896]{2,1,0:T(4,128)(2,1)} %convert_element_type.96), calls=%async_computation.4 | async-start | bytes 458752 | tf_op jit(solution)/shard_map/all_to_all | solution.py:155
  310.4 3.1 fusion.37
  313.5 0.5 copy-done.1
  314.1 1.6 slice.47
  315.7 4.4 %reshape_reshape.13 = bf16[896,1344]{1,0:T(8,128)(2,1)} reshape(bf16[16,75264]{1,0:T(8,128)(2,1)} %slice.47) | data formatting | bytes 4816896 | tf_op jit(solution)/shard_map/reshape;reshape | solution.py:16
  320.0 3.2 reshape_reshape.14
  323.3 3.2 reshape_reshape.15
  326.4 2.1 reshape_reshape.16
  328.6 0.0 all-to-all-done.2
  328.6 0.1 reshape.271
  328.6 0.3 multiply_reduce_fusion.1
  329.0 2.8 fusion.2
  331.9 0.3 convolution_multiply_fusion
  332.1 0.9 fusion.40
  333.1 1.0 convolution_convert_fusion.6
  334.0 1.6 multiply_reduce_fusion
  335.6 1.7 convolution_convert_fusion.4
  337.3 0.2 convolution_multiply_fusion.1
  337.5 0.2 fusion.41
  337.7 0.2 convolution_convert_fusion.5
  337.9 2.2 fusion.9
  (24 shorter events, 0.1 us)
Async XLA Ops:
  7.4 50.2 %copy-start = (bf16[4000,256]{1,0:T(8,128)(2,1)S(1)}, bf16[4000,256]{1,0:T(8,128)(2,1)}, u32[]{:S(2)}) copy-start(bf16[4000,256]{1,0:T(8,128)(2,1)} %param.13) | copy-start | bytes 6144004
  29.1 28.4 %all-to-all-start.1 = ((s32[16,1,128]{2,1,0:T(1,128)}), s32[16,1,128]{2,1,0:T(1,128)S(1)}, u32[]{:S(2)}, u32[]{:S(2)}) async-start(s32[16,1,128]{2,1,0:T(1,128)} %broadcast_in_dim.66), calls=%async_computation.1 | async-start | bytes 16384 | tf_op jit(solution)/shard_map/all_to_all | solution.py:21
  44.0 108.7 %reduce-scatter.3.cloned.1.call-start = ((), (), s32[]{:S(2)}) async-start(), calls=%async_computation.7 | async-start | bytes 4587520 | tf_op jit(solution)/shard_map/reduce_scatter | solution.py:31
  69.0 0.9 copy-start.4
  69.0 1.1 copy-start.5
  69.0 1.2 copy-start.6
  69.0 1.3 copy-start.7
  69.0 2.2 copy-start.2
  69.0 2.2 copy-start.3
  69.1 220.9 %all-gather.3.cloned.1.call-start = ((), (), s32[]{:S(2)}) async-start(), calls=%async_computation.9 | async-start | bytes 5117952 | tf_op jit(solution)/shard_map/all_gather | solution.py:61
  137.9 56.9 %all-to-all-start.4 = ((bf16[16,32,896]{2,1,0:T(8,128)(2,1)}), bf16[16,32,896]{2,1,0:T(8,128)(2,1)S(1)}, u32[]{:S(2)}, u32[]{:S(2)}) async-start(bf16[16,32,896]{2,1,0:T(8,128)(2,1)} %broadcast_in_dim.73), calls=%async_computation.6 | async-start | bytes 1835008 | tf_op jit(solution)/shard_map/all_to_all | solution.py:21
  152.6 142.6 %reduce-scatter.5.cloned.1.call-start = ((), (), s32[]{:S(2)}) async-start(), calls=%async_computation.8 | async-start | bytes 1146880 | tf_op jit(solution)/shard_map/reduce_scatter | solution.py:31
  296.9 31.7 %all-to-all-start.2 = ((bf16[32,4,896]{2,1,0:T(4,128)(2,1)}), bf16[32,4,896]{2,1,0:T(4,128)(2,1)S(1)}, u32[]{:S(2)}, u32[]{:S(2)}) async-start(bf16[32,4,896]{2,1,0:T(4,128)(2,1)} %convert_element_type.96), calls=%async_computation.4 | async-start | bytes 458752 | tf_op jit(solution)/shard_map/all_to_all | solution.py:155
  310.4 3.6 %copy-start.1 = (bf16[16,150528]{1,0:T(8,128)(2,1)S(1)}, bf16[16,150528]{1,0:T(8,128)(2,1)}, u32[]{:S(2)}) copy-start(bf16[16,150528]{1,0:T(8,128)(2,1)} %reshape.322) | copy-start | bytes 14450692
  323.2 5.7 %copy-start.8 = (f32[896]{0:T(1024)S(1)}, f32[896]{0:T(1024)}, u32[]{:S(2)}) copy-start(f32[896]{0:T(1024)} %param.16) | copy-start | bytes 10756
  333.1 2.5 copy-start.9
Sparse Core Ops, SparseCore 0:
  69.2 48.6 reduce-scatter.2
  156.2 126.0 reduce-scatter.4
Sparse Core Ops, SparseCore 1:
  72.6 217.3 all-gather.2
where the time goes:
time: 348 us
  waiting for transfers between devices  150 us (43%)
  blocking collectives  82.1 us (24%)
  starting transfers between devices  43.2 us (12%)
  local copies, waits for them, and re-layouts  36.6 us (11%)
  matrix products  15.7 us (5%)
  between operations  15.2 us (4%)
  other arithmetic  4.33 us (1%)
    all_gather x1, waiting for transfers between devices, gather_together(): lines, at, finished = (lax.all_gather(flat, axis), 0, [])  94.8 us
    all_to_all x1, blocking collectives, summed_on_arrival(): lax.all_to_all(parts, axis, split_axis=0, concat_axis=0, tiled=True)  65.1 us
    all_to_all x2, waiting for transfers between devices, copy_for_each(): return lax.all_to_all(copies, axis, split_axis=0, concat_axis=0, tiled=True)  55 us
    all_to_all x2, starting transfers between devices, copy_for_each(): return lax.all_to_all(copies, axis, split_axis=0, concat_axis=0, tiled=True)  29.5 us
    all_to_all x1, blocking collectives, body(): lax.all_to_all(outgoing, 'vocab', split_axis=0, concat_axis=0, tiled=True)  17 us
    all_to_all x1, starting transfers between devices, body(): lax.all_to_all(slot_rows.reshape(shards, room, enc_width), 'vocab', split...  13.5 us
    another operation x4, local copies, waits for them, and re-layouts, joined_along(): parts.reshape(*dims[:dim], dims[dim] * dims[dim + 1], *dims[dim + 2:])  12.9 us
    gather x1, local copies, waits for them, and re-layouts, body(): looked = jnp.take(table, jnp.clip(local_row, 0, table_rows - 1), axis=0)  7.5 us
  transfers between devices with their start and end apart: 6, of which 3 were waited for; matrix products, arithmetic and copies ran while one was open for 7% of the time, Pallas kernels for 0%

commit v1 on v0

v1 whole, which is shorter than its diff:
```python
import functools

import jax
import jax.numpy as jnp
from jax import lax
from jax.experimental import pallas as pl
from jax.experimental.pallas import tpu as pltpu
from jax.sharding import PartitionSpec as P

MESH = pl.DeviceIdType.MESH
BF = jnp.bfloat16
F32 = jnp.float32
HEAD = 64
NV = 32
NB = 16
QK_AT, V_AT, CQ_AT, SO_AT, CO_AT = 0, 56, 84, 112, 140
PIECE = 24
VMEM_LIMIT = 60 * 1024 * 1024


def where_am_i():
    v = lax.axis_index("vocab")
    b = lax.axis_index("batch")
    return v, b, v // 8, lax.rem(v, 2), b // 4, lax.rem(b, 4)


def send(src, dst, ssem, rsem, dev):
    return pltpu.make_async_remote_copy(
        src_ref=src, dst_ref=dst, send_sem=ssem, recv_sem=rsem,
        device_id=dev, device_id_type=MESH,
    )


def greet(v, b, all_batch):
    barrier = pltpu.get_barrier_semaphore()

    def hello_vocab(o, _):
        pl.semaphore_signal(
            barrier, inc=1, device_id=(lax.rem(v + o, NV), b), device_id_type=MESH
        )
        return 0

    lax.fori_loop(1, NV, hello_vocab, 0)
    if all_batch:
        def hello_batch(o, _):
            pl.semaphore_signal(
                barrier, inc=1, device_id=(v, lax.rem(b + o, NB)), device_id_type=MESH
            )
            return 0

        lax.fori_loop(1, NB, hello_batch, 0)
        pl.semaphore_wait(barrier, NV - 1 + NB - 1)
    else:
        y, z = b // 4, lax.rem(b, 4)
        for dy, dz in ((1, 0), (3, 0), (0, 1), (0, 3)):
            peer = lax.rem(y + dy, 4) * 4 + lax.rem(z + dz, 4)
            pl.semaphore_signal(barrier, inc=1, device_id=(v, peer), device_id_type=MESH)
        pl.semaphore_wait(barrier, NV - 1 + 4)


class RingSum:
    def __init__(self, chunk, got, ssem, rsem, ahead, behind):
        def m(i, src, dev):
            return send(src, got.at[i], ssem.at[i], rsem.at[i], dev)

        self.chunk, self.got = chunk, got
        self.opp_a = m(0, chunk(2, 0), ahead)
        self.opp_b = m(1, chunk(2, 1), behind)
        self.next_b = m(2, chunk(1, 1), ahead)
        self.prev_a = m(3, chunk(3, 0), behind)
        self.merged_a = m(4, chunk(1, 0), ahead)
        self.merged_b = m(5, chunk(3, 1), behind)

    def merge_a(self):
        self.opp_a.wait_recv()
        ref = self.chunk(1, 0)
        ref[...] = (ref[...].astype(F32) + self.got[0].astype(F32)).astype(BF)
        self.merged_a.start()

    def merge_b(self):
        self.opp_b.wait_recv()
        ref = self.chunk(3, 1)
        ref[...] = (ref[...].astype(F32) + self.got[1].astype(F32)).astype(BF)
        self.merged_b.start()

    def total(self):
        self.prev_a.wait_recv()
        self.merged_a.wait_recv()
        a = self.chunk(0, 0)[...].astype(F32) + self.got[3].astype(F32) + self.got[4].astype(F32)
        self.next_b.wait_recv()
        self.merged_b.wait_recv()
        b = self.chunk(0, 1)[...].astype(F32) + self.got[2].astype(F32) + self.got[5].astype(F32)
        return a, b

    def drain(self):
        for c in (self.opp_a, self.opp_b, self.next_b, self.prev_a, self.merged_a, self.merged_b):
            c.wait_send()


class RingCopies:
    def __init__(self, own, slot, half, me, ssem, rsem, ahead, behind):
        left, right = lax.rem(me + 3, 4), lax.rem(me + 1, 4)
        far = lax.rem(me + 2, 4)
        self.to_ahead = send(own, slot(me), ssem.at[0], rsem.at[0], ahead)
        self.to_behind = send(own, slot(me), ssem.at[1], rsem.at[1], behind)
        self.on_ahead = send(half(left, 0), half(left, 0), ssem.at[2], rsem.at[2], ahead)
        self.on_behind = send(half(right, 1), half(right, 1), ssem.at[3], rsem.at[3], behind)
        self.from_left = (slot(left), rsem.at[0])
        self.from_right = (slot(right), rsem.at[1])
        self.far_a = (half(far, 0), rsem.at[2])
        self.far_b = (half(far, 1), rsem.at[3])

    def start(self):
        self.to_ahead.start()
        self.to_behind.start()

    def forward(self):
        self.to_ahead.wait_recv()
        self.on_ahead.start()
        self.to_behind.wait_recv()
        self.on_behind.start()

    def finish(self):
        self.on_ahead.wait_recv()
        self.on_behind.wait_recv()

    def drain(self):
        for c in (self.to_ahead, self.to_behind, self.on_ahead, self.on_behind):
            c.wait_send()


def packed_rows(start, count):
    done = 0
    while done < count:
        at = start + done
        take = min(count - done, PIECE - at % PIECE)
        yield done, at // PIECE, at % PIECE, take
        done += take


def first_kernel(
    ids_ref, q_ref, kvp_ref, qkv_ref, so_ref, cq_ref, co_ref,
    wanted_ref, span_ref, wg_out_ref,
    ids_got, row_ref, rows_got, pack, wg, kv_chunk, kv_got, kv_y, kv_in,
    ids_s, ids_r, row_s, row_r, wz_s, wz_r, wy_s, wy_r, ky_s, ky_r, kz_s, kz_r,
):
    v, b, x, c, y, z = where_am_i()
    greet(v, b, True)

    def ask(o, _):
        to = lax.rem(v + o, NV)
        send(ids_ref.at[to], ids_got.at[v], ids_s.at[o], ids_r.at[o], (to, b)).start()
        return 0

    lax.fori_loop(1, NV, ask, 0)

    def put(block, start, lanes):
        for at, piece, row, take in packed_rows(start, block.shape[0]):
            pack[piece, row : row + take, lanes] = block[at : at + take]

    whole = slice(0, 896)
    put(qkv_ref[:, 0:896], QK_AT, whole)
    put(jnp.concatenate([qkv_ref[0:28, 896:1344], qkv_ref[28:56, 896:1344]], axis=1), V_AT, whole)
    put(jnp.concatenate([cq_ref[0:28, :], cq_ref[28:56, :]], axis=1), CQ_AT, whole)
    put(so_ref[...], SO_AT, whole)
    put(co_ref[...], CO_AT, whole)
    pack[7] = jnp.zeros_like(pack[7])
    member = x * 2 + c
    wz = []
    for o in (2, 1, 3):
        wz.append(
            send(pack.at[member], wg.at[y, z], wz_s.at[o - 1], wz_r.at[o - 1],
                 (v, y * 4 + lax.rem(z + o, 4)))
        )
        wz[-1].start()
    wg[y, z] = pack[member]

    ahead = (v, lax.rem(y + 1, 4) * 4 + z)
    behind = (v, lax.rem(y + 3, 4) * 4 + z)
    ky = RingSum(lambda r, h: kv_chunk.at[r, h], kv_got, ky_s, ky_r, ahead, behind)
    for r in (2, 1, 3, 0):
        term = jnp.dot(q_ref[lax.rem(y + r, 4)], kvp_ref[...], preferred_element_type=F32)
        kv_chunk[r] = term.reshape(2, 64, 896).astype(BF)
        if r == 2:
            ky.opp_a.start()
            ky.opp_b.start()
        elif r == 1:
            ky.next_b.start()
        elif r == 3:
            ky.prev_a.start()

    def asked(o, _):
        send(ids_ref.at[v], ids_got.at[v], ids_s.at[o], ids_r.at[o], (v, b)).wait_recv()
        return 0

    lax.fori_loop(1, NV, asked, 0)
    ids_got[v] = ids_ref[v]
    row_ref[...] = jnp.sum(ids_got[...], axis=0)

    def tell(o, _):
        to = lax.rem(b + o, NB)
        send(row_ref, rows_got.at[b], row_s.at[o], row_r.at[o], (v, to)).start()
        return 0

    lax.fori_loop(1, NB, tell, 0)
    rows_got[b] = row_ref[...]

    ky.merge_a()
    ky.merge_b()
    for copy in wz:
        copy.wait_recv()
    wy = RingCopies(
        wg.at[y], lambda i: wg.at[i], lambda i, h: wg.at[i, pl.ds(2 * h, 2)], y, wy_s, wy_r, ahead, behind
    )
    wy.start()
    a, bb = ky.total()
    kv_y[0] = a.astype(BF)
    kv_y[1] = bb.astype(BF)
    mine = z // 2
    odd = lax.rem(z, 2)
    outside = (v, y * 4 + lax.rem(z + 3 + 2 * odd, 4))
    kz = send(kv_y.at[1 - mine], kv_in, kz_s, kz_r, outside)
    kz.start()
    wy.forward()

    def told(o, _):
        send(row_ref, rows_got.at[b], row_s.at[o], row_r.at[o], (v, b)).wait_recv()
        return 0

    lax.fori_loop(1, NB, told, 0)
    wanted_ref[...] = rows_got[:, 0, :]
    kz.wait_recv()
    span_ref[...] = (kv_y[mine].astype(F32) + kv_in[...].astype(F32)).astype(BF)
    wy.finish()
    for i in range(4):
        wg_out_ref[pl.ds(4 * i, 4)] = wg[i]

    def sent_ids(o, _):
        send(ids_ref.at[v], ids_got.at[v], ids_s.at[o], ids_r.at[o], (v, b)).wait_send()
        return 0

    lax.fori_loop(1, NV, sent_ids, 0)

    def sent_rows(o, _):
        send(row_ref, rows_got.at[b], row_s.at[o], row_r.at[o], (v, b)).wait_send()
        return 0

    lax.fori_loop(1, NB, sent_rows, 0)
    for copy in wz:
        copy.wait_send()
    wy.drain()
    ky.drain()
    kz.wait_send()


def normed(values, gain):
    scale = lax.rsqrt(jnp.mean(values * values, axis=-1, keepdims=True) + 1e-06)
    return (values * scale * gain).astype(BF)


def softmax(scores):
    e = jnp.exp(scores - jnp.max(scores, axis=-1, keepdims=True))
    return (e / jnp.sum(e, axis=-1, keepdims=True)).astype(BF)


def attend(queries, keys, values):
    outs = []
    for h in range(queries.shape[1] // HEAD):
        cut = slice(h * HEAD, (h + 1) * HEAD)
        scores = lax.dot_general(
            queries[:, cut], keys[:, cut], (((1,), (1,)), ((), ())), preferred_element_type=F32
        ) * HEAD ** (-0.5)
        outs.append(jnp.dot(softmax(scores), values[:, cut], preferred_element_type=F32).astype(BF))
    return jnp.concatenate(outs, axis=1)


def second_kernel(
    looked_ref, inp_ref, sel_ref, span_ref, wg_ref, ns_ref, nc_ref,
    out_ref,
    chunk, y_got, z_chunk, z_got, sums, back_out, back_in, back_rows, full, mate_span,
    w_qk, w_v, w_cq, w_so, w_co,
    y_s, y_r, z_s, z_r, back_s, back_r, wx_s, wx_r, wc_s, wc_r, m_s, m_r,
):
    v, b, x, c, y, z = where_am_i()
    greet(v, b, False)
    ahead = (v, lax.rem(y + 1, 4) * 4 + z)
    behind = (v, lax.rem(y + 3, 4) * 4 + z)
    z_ahead = (v, y * 4 + lax.rem(z + 1, 4))
    z_behind = (v, y * 4 + lax.rem(z + 3, 4))
    rest = lax.rem(v, 8)
    x_ahead = (lax.rem(x + 1, 4) * 8 + rest, b)
    x_behind = (lax.rem(x + 3, 4) * 8 + rest, b)
    odd = lax.rem(z, 2)
    z_mate = (v, y * 4 + z + 1 - 2 * odd)
    mate = (v + 1 - 2 * c, b)

    spans = send(span_ref, mate_span, m_s, m_r, z_mate)
    spans.start()
    wx = RingCopies(
        wg_ref, lambda i: full.at[c, i], lambda i, h: full.at[c, i, pl.ds(8 * h, 8)], x,
        wx_s, wx_r, x_ahead, x_behind,
    )
    wx.start()

    order = (2, 1, 3, 0)
    sums_y = []
    for k, rz in enumerate(order):
        ring = RingSum(
            lambda r, h, k=k: chunk.at[k, r, h], y_got.at[k], y_s.at[k], y_r.at[k], ahead, behind
        )
        sums_y.append(ring)
        for r in order:
            peer = lax.rem(y + r, 4) * 4 + lax.rem(z + rz, 4)
            term = jnp.dot(looked_ref[peer], inp_ref[...], preferred_element_type=F32)
            chunk[k, r] = term.reshape(2, 64, 896).astype(BF)
            if r == 2:
                ring.opp_a.start()
                ring.opp_b.start()
            elif r == 1:
                ring.next_b.start()
            elif r == 3:
                ring.prev_a.start()

    to_mate = []

    def pass_on(i, src, dst):
        copy = send(src, dst, wc_s.at[i], wc_r.at[i], mate)
        copy.start()
        to_mate.append(copy)

    pass_on(0, wg_ref, full.at[c, x])
    full[c, x] = wg_ref[...]

    zsum = RingSum(lambda r, h: z_chunk.at[r, h], z_got, z_s, z_r, z_ahead, z_behind)

    def settle(k):
        a, bb = sums_y[k].total()
        z_chunk[order[k], 0] = a.astype(BF)
        z_chunk[order[k], 1] = bb.astype(BF)

    def merge(k):
        sums_y[k].merge_a()
        sums_y[k].merge_b()

    merge(0)
    merge(1)
    settle(0)
    zsum.opp_a.start()
    zsum.opp_b.start()
    merge(2)
    settle(1)
    zsum.next_b.start()
    wx.forward()
    for i, o in ((1, 3), (2, 1)):
        slot = full.at[c, lax.rem(x + o, 4)]
        pass_on(i, slot, slot)
    merge(3)
    settle(2)
    zsum.prev_a.start()
    zsum.merge_a()
    zsum.merge_b()
    settle(3)
    wx.finish()
    slot = full.at[c, lax.rem(x + 2, 4)]
    pass_on(3, slot, slot)

    for copy in to_mate:
        copy.wait_recv()

    def rows_of(bb, start, count):
        parts = []
        for _, piece, row, take in packed_rows(start, count):
            parts.append(full[piece % 2, piece // 2, bb, row : row + take, :])
        return parts

    def lay(dst, at, parts, lanes):
        for part in parts:
            dst[at : at + part.shape[0], :] = part[:, lanes]
            at += part.shape[0]

    whole = slice(0, 896)
    for bb in range(NB):
        lay(w_qk, 56 * bb, rows_of(bb, QK_AT, 56), whole)
        for dst, start in ((w_v, V_AT), (w_cq, CQ_AT)):
            parts = rows_of(bb, start, 28)
            lay(dst, 56 * bb, parts, slice(0, 448))
            lay(dst, 56 * bb + 28, parts, slice(448, 896))
        lay(w_so, 28 * bb, rows_of(bb, SO_AT, 28), whole)
        lay(w_co, 28 * bb, rows_of(bb, CO_AT, 28), whole)

    a, bb = zsum.total()
    sums[0:64] = a
    sums[64:128] = bb
    for i in range(NV):
        back_out[i] = sums[4 * i : 4 * i + 4, :].astype(BF)

    def give(o, _):
        to = lax.rem(v + o, NV)
        send(back_out.at[to], back_in.at[v], back_s.at[o], back_r.at[o], (to, b)).start()
        return 0

    lax.fori_loop(1, NV, give, 0)
    back_in[v] = back_out[v]

    def given(o, _):
        send(back_out.at[v], back_in.at[v], back_s.at[o], back_r.at[o], (v, b)).wait_recv()
        return 0

    lax.fori_loop(1, NV, given, 0)
    for i in range(NV):
        back_rows[4 * i : 4 * i + 4, :] = back_in[i].astype(F32)
    start = jnp.dot(sel_ref[...], back_rows[...].astype(BF), preferred_element_type=F32)
    stream = start.astype(BF).astype(F32)

    self_in = normed(stream, ns_ref[...])
    qk = jnp.dot(self_in, w_qk[...], preferred_element_type=F32).astype(BF)
    vals = jnp.dot(self_in, w_v[...], preferred_element_type=F32).astype(BF)
    heads = attend(qk[:, 0:448], qk[:, 448:896], vals)
    stream = stream + jnp.dot(heads, w_so[...], preferred_element_type=F32)
    cross_in = normed(stream, nc_ref[...])
    cross_q = jnp.dot(cross_in, w_cq[...], preferred_element_type=F32).astype(BF)
    spans.wait_recv()
    span_kv = (span_ref[...].astype(F32) + mate_span[...].astype(F32)).astype(BF)
    heads = attend(cross_q, span_kv[:, 0:448], span_kv[:, 448:896])
    stream = stream + jnp.dot(heads, w_co[...], preferred_element_type=F32)
    out_ref[...] = stream.astype(BF)

    def gone(o, _):
        send(back_out.at[v], back_in.at[v], back_s.at[o], back_r.at[o], (v, b)).wait_send()
        return 0

    lax.fori_loop(1, NV, gone, 0)
    for ring in sums_y:
        ring.drain()
    zsum.drain()
    wx.drain()
    for copy in to_mate:
        copy.wait_send()
    spans.wait_send()


def vmem(n):
    return [pl.BlockSpec(memory_space=pltpu.VMEM)] * n


DMA = pltpu.SemaphoreType.DMA


def body(
    neighbour_ids, query_states, table, in_proj, kv_proj, norm_self, self_qkv, self_out,
    norm_cross, cross_q, cross_out,
):
    me = lax.axis_index("vocab")
    table_rows = table.shape[0]
    ids = neighbour_ids.reshape(-1)
    owner = ids // table_rows
    earlier = jnp.arange(128)[:, None] > jnp.arange(128)[None, :]
    within = jnp.sum((owner[:, None] == owner[None, :]) & earlier, axis=1, dtype=jnp.int32)
    slot = owner * 4 + within
    lanes = jnp.arange(128, dtype=jnp.int32)
    selector = (slot[:, None] == lanes[None, :]).astype(BF)
    mine = (owner[:, None] == jnp.arange(NV, dtype=jnp.int32)[None, :])[:, :, None]
    here = ((4 * me + within)[:, None] == lanes[None, :])[:, None, :]
    asks = jnp.sum(jnp.where(mine & here, ids[:, None, None] + 1, 0), axis=0)

    wanted, span, wg = pl.pallas_call(
        first_kernel,
        out_shape=[
            jax.ShapeDtypeStruct((NB, 128), jnp.int32),
            jax.ShapeDtypeStruct((64, 896), BF),
            jax.ShapeDtypeStruct((NB, PIECE, 896), BF),
        ],
        in_specs=vmem(7),
        out_specs=vmem(3),
        scratch_shapes=[
            pltpu.VMEM((NV, 1, 128), jnp.int32),
            pltpu.VMEM((1, 128), jnp.int32),
            pltpu.VMEM((NB, 1, 128), jnp.int32),
            pltpu.VMEM((8, PIECE, 896), BF),
            pltpu.VMEM((4, 4, PIECE, 896), BF),
            pltpu.VMEM((4, 2, 64, 896), BF),
            pltpu.VMEM((6, 64, 896), BF),
            pltpu.VMEM((2, 64, 896), BF),
            pltpu.VMEM((64, 896), BF),
            DMA((NV,)), DMA((NV,)), DMA((NB,)), DMA((NB,)), DMA((3,)), DMA((3,)),
            DMA((4,)), DMA((4,)), DMA((6,)), DMA((6,)), DMA, DMA,
        ],
        compiler_params=pltpu.CompilerParams(
            collective_id=0, has_side_effects=True, vmem_limit_bytes=VMEM_LIMIT
        ),
        name="first",
    )(asks.reshape(NV, 1, 128), query_states.reshape(4, 128, 256), kv_proj, self_qkv, self_out, cross_q, cross_out)

    rows = jnp.clip(wanted - 1 - me * table_rows, 0, table_rows - 1)
    looked = jnp.take(table, rows, axis=0)

    out = pl.pallas_call(
        second_kernel,
        out_shape=jax.ShapeDtypeStruct((128, 896), BF),
        in_specs=vmem(7),
        out_specs=vmem(1)[0],
        scratch_shapes=[
            pltpu.VMEM((4, 4, 2, 64, 896), BF),
            pltpu.VMEM((4, 6, 64, 896), BF),
            pltpu.VMEM((4, 2, 64, 896), BF),
            pltpu.VMEM((6, 64, 896), BF),
            pltpu.VMEM((128, 896), F32),
            pltpu.VMEM((NV, 4, 896), BF),
            pltpu.VMEM((NV, 4, 896), BF),
            pltpu.VMEM((128, 896), F32),
            pltpu.VMEM((2, 4, NB, PIECE, 896), BF),
            pltpu.VMEM((64, 896), BF),
            pltpu.VMEM((896, 896), BF),
            pltpu.VMEM((896, 448), BF),
            pltpu.VMEM((896, 448), BF),
            pltpu.VMEM((448, 896), BF),
            pltpu.VMEM((448, 896), BF),
            DMA((4, 6)), DMA((4, 6)), DMA((6,)), DMA((6,)), DMA((NV,)), DMA((NV,)),
            DMA((4,)), DMA((4,)), DMA((4,)), DMA((4,)), DMA, DMA,
        ],
        compiler_params=pltpu.CompilerParams(
            collective_id=1, has_side_effects=True, vmem_limit_bytes=VMEM_LIMIT
        ),
        name="second",
    )(looked, in_proj, selector, span, wg, norm_self.reshape(1, 896), norm_cross.reshape(1, 896))
    return out.reshape(1, 128, 896)


def solution(mesh):
    both = ("vocab", "batch")
    in_specs = (
        P(both, None), P("vocab", None, "batch"), P("vocab", "batch"), P("batch", None),
        P("batch", None), P(), P("batch", None), P("batch", None), P(), P("batch", None),
        P("batch", None),
    )
    return jax.shard_map(
        body, mesh=mesh, in_specs=in_specs, out_specs=P(both, None, None), check_vma=False
    )
```

time: 348 us -> 140 us (0.40)
  waiting for transfers between devices: 150 us -> 0 us
  Pallas kernels: 0 us -> 123 us
  blocking collectives: 82.1 us -> 0 us
  starting transfers between devices: 43.2 us -> 0 us
  local copies, waits for them, and re-layouts: 36.6 us -> 10.4 us
  matrix products: 15.7 us -> 0 us
  between operations: 15.2 us -> 0.1 us
    pallas_call x0 -> x2, Pallas kernels: none -> 123 us  [the longest x1 80.9 us: body(): pl.pallas_call(second_kernel, out_shape=jax.ShapeDtypeStruct((128, 896),...]
    all_gather x1 -> x0, waiting for transfers between devices: 94.8 us -> none  [gather_together(): lines, at, finished = (lax.all_gather(flat, axis), 0, [])]
    all_to_all x2 -> x0, blocking collectives: 82.1 us -> none  [the longest x1 65.1 us: summed_on_arrival(): lax.all_to_all(parts, axis, split_axis=0, concat_axis=0, tiled=True)]
    all_to_all x3 -> x0, waiting for transfers between devices: 55 us -> none  [the longest x2 55 us: copy_for_each(): return lax.all_to_all(copies, axis, split_axis=0, concat_axis=0, tiled=True)]
    all_to_all x3 -> x0, starting transfers between devices: 43.1 us -> none  [the longest x2 29.5 us: copy_for_each(): return lax.all_to_all(copies, axis, split_axis=0, concat_axis=0, tiled=True)]
    dot_general x11 -> x0, matrix products: 14.5 us -> none  [the longest x1 3.9 us: body(): jnp.einsum('bsd,de->bse', looked, in_proj, preferred_element_type=jnp.flo...]
    another operation x5 -> x0, local copies, waits for them, and re-layouts: 13 us -> none  [the longest x4 12.9 us: joined_along(): parts.reshape(*dims[:dim], dims[dim] * dims[dim + 1], *dims[dim + 2:])]
    all_gather x1 -> x0, local copies, waits for them, and re-layouts: 5.22 us -> none  [gather_together(): lines, at, finished = (lax.all_gather(flat, axis), 0, [])]
  transfers between devices with their start and end apart: 6 -> 0, of which waited for: 3 -> 0; matrix products, arithmetic and copies ran while one was open for 7% -> 0% of each run, Pallas kernels for 0% -> 0%
where the time goes in v1:
time: 140 us
  Pallas kernels  123 us (88%)
  local copies, waits for them, and re-layouts  10.4 us (7%)
  other arithmetic  6.04 us (4%)
    pallas_call x1, Pallas kernels, body(): pl.pallas_call(second_kernel, out_shape=jax.ShapeDtypeStruct((128, 896),...  80.9 us
    pallas_call x1, Pallas kernels, body(): pl.pallas_call(first_kernel, out_shape=[jax.ShapeDtypeStruct((NB, 128), j...  42.2 us
    gather x1, local copies, waits for them, and re-layouts, body(): looked = jnp.take(table, rows, axis=0)  7.5 us

profile of v1, /device:TPU:1, one launch (start us, length us, event | category | flops | bytes accessed | tf_op | source)
XLA Modules:
  0.0 139.6 jit_solution(12839351195370685485)
XLA Ops:
  0.0 0.0 copy-start
  0.0 0.8 bitcast_select_fusion
  0.8 0.7 fusion.2
  1.5 0.2 convert_reduce_fusion
  1.7 0.7 iota_compare_fusion.1
  2.4 0.1 iota_compare_fusion.3
  2.5 1.6 %select_reduce_fusion = s32[32,128]{1,0:T(8,128)} fusion(s32[128]{0:T(128)S(1)} %get-tuple-element.16, pred[128,128]{1,0:T(8,128)(4,1)S(1)} %get-tuple-element.17, pred[128,32]{1,0:T(8,128)(4,1)S(1)} %iota_compare_fusion.3), kind=kLoop, calls=%fused_computation.1 | loop fusion | flops 1568768 | bytes 37376 | tf_op jit(solution)/shard_map/reduce_sum | solution.py:464
  4.1 42.2 %first.1 = (s32[16,128]{1,0:T(8,128)}, bf16[64,896]{1,0:T(8,128)(2,1)}, bf16[16,24,896]{2,1,0:T(8,128)(2,1)}) custom-call(s32[32,1,128]{2,1,0:T(1,128)} %bitcast.17, bf16[4,128,256]{2,1,0:T(8,128)(2,1)} %bitcast.16, bf16[256,896]{1,0:T(8,128)(2,1)} %kvp_ref.1, bf16[56,1344]{1,0:T(8,128)(2,1)} %qkv_ref.1, bf16[28,896]{1,0:T(8,128)(2,1)} %so_ref.1, ...), custom_call_target="tpu_custom_call" | custom-call | tf_op jit(solution)/shard_map/first/pallas_call | solution.py:466
  46.3 0.7 bitcast_clamp_fusion
  47.1 0.0 copy-done
  47.1 0.0 copy-start.1
  47.1 7.5 %gather_fusion = bf16[2048,256]{1,0:T(8,128)(2,1)S(1)} fusion(bf16[4000,256]{1,0:T(8,128)(2,1)S(1)} %copy-done, s32[2048]{0:T(1024)S(1)} %bitcast_clamp_fusion), kind=kCustom, calls=%fused_computation | custom fusion | bytes 2105344 | tf_op jit(solution)/shard_map/jit(_take)/gather | solution.py:495
  54.6 0.0 copy-start.2
  54.6 0.0 copy-start.3
  54.6 0.0 copy-done.1
  54.6 1.2 broadcast_select_fusion.looked_ref
  55.9 0.0 copy-done.2
  55.9 0.6 reshape.111.ns_ref
  56.4 0.0 copy-done.3
  56.5 0.6 reshape.112.nc_ref
  57.0 80.9 %second.1 = bf16[128,896]{1,0:T(8,128)(2,1)} custom-call(bf16[16,128,256]{2,1,0:T(8,128)(2,1)} %broadcast_select_fusion.looked_ref, bf16[256,896]{1,0:T(8,128)(2,1)} %inp_ref.1, bf16[128,128]{1,0:T(8,128)(2,1)} %get-tuple-element.18.sel_ref, bf16[64,896]{1,0:T(8,128)(2,1)} %get-tuple-element.9.span_ref, bf16[16,24,896]{2,1,0:T(8,128)(2,1)} %get-tuple-element.10.wg_ref, ...), custom_call_target="tpu_custom_call" | custom-call | tf_op jit(solution)/shard_map/second/pallas_call | solution.py:497
  137.9 1.6 %copy.13 = bf16[1,128,896]{2,1,0:T(8,128)(2,1)} copy(bf16[1,128,896]{2,1,0:T(8,128)(2,1)} %bitcast.15) | data formatting | bytes 458752
  (2 shorter events, 0.0 us)
Async XLA Ops:
  0.0 47.1 %copy-start = (bf16[4000,256]{1,0:T(8,128)(2,1)S(1)}, bf16[4000,256]{1,0:T(8,128)(2,1)}, u32[]{:S(2)}) copy-start(bf16[4000,256]{1,0:T(8,128)(2,1)} %param.13) | copy-start | bytes 6144004
  47.1 7.5 %copy-start.1 = (s32[16,128]{1,0:T(8,128)S(1)}, s32[16,128]{1,0:T(8,128)}, u32[]{:S(2)}) copy-start(s32[16,128]{1,0:T(8,128)} %get-tuple-element.8) | copy-start | bytes 24580
  54.6 1.3 copy-start.2
  54.6 1.9 %copy-start.3 = (f32[896]{0:T(1024)S(1)}, f32[896]{0:T(1024)}, u32[]{:S(2)}) copy-start(f32[896]{0:T(1024)} %param.19) | copy-start | bytes 10756

commit v2 on v1

v2 whole, which is shorter than its diff:
```python
import functools

import jax
import jax.numpy as jnp
from jax import lax
from jax.experimental import pallas as pl
from jax.experimental.pallas import tpu as pltpu
from jax.sharding import PartitionSpec as P

MESH = pl.DeviceIdType.MESH
BF = jnp.bfloat16
F32 = jnp.float32
HEAD = 64
NV = 32
NB = 16
QK_AT, V_AT, CQ_AT, SO_AT, CO_AT = 0, 56, 84, 112, 140
PIECE = 24
VMEM_LIMIT = 60 * 1024 * 1024


def where_am_i():
    v = lax.axis_index("vocab")
    b = lax.axis_index("batch")
    return v, b, v // 8, lax.rem(v, 2), b // 4, lax.rem(b, 4)


def send(src, dst, ssem, rsem, dev):
    return pltpu.make_async_remote_copy(
        src_ref=src, dst_ref=dst, send_sem=ssem, recv_sem=rsem,
        device_id=dev, device_id_type=MESH,
    )


def greet(v, b):
    barrier = pltpu.get_barrier_semaphore()

    def hello_vocab(o, _):
        pl.semaphore_signal(
            barrier, inc=1, device_id=(lax.rem(v + o, NV), b), device_id_type=MESH
        )
        return 0

    lax.fori_loop(1, NV, hello_vocab, 0)

    def hello_batch(o, _):
        pl.semaphore_signal(
            barrier, inc=1, device_id=(v, lax.rem(b + o, NB)), device_id_type=MESH
        )
        return 0

    lax.fori_loop(1, NB, hello_batch, 0)


def all_here():
    pl.semaphore_wait(pltpu.get_barrier_semaphore(), NV - 1 + NB - 1)


class RingSum:
    def __init__(self, chunk, got, ssem, rsem, ahead, behind):
        def m(i, src, dev):
            return send(src, got.at[i], ssem.at[i], rsem.at[i], dev)

        self.chunk, self.got = chunk, got
        self.opp_a = m(0, chunk(2, 0), ahead)
        self.opp_b = m(1, chunk(2, 1), behind)
        self.next_b = m(2, chunk(1, 1), ahead)
        self.prev_a = m(3, chunk(3, 0), behind)
        self.merged_a = m(4, chunk(1, 0), ahead)
        self.merged_b = m(5, chunk(3, 1), behind)

    def merge_a(self):
        self.opp_a.wait_recv()
        ref = self.chunk(1, 0)
        ref[...] = (ref[...].astype(F32) + self.got[0].astype(F32)).astype(BF)
        self.merged_a.start()

    def merge_b(self):
        self.opp_b.wait_recv()
        ref = self.chunk(3, 1)
        ref[...] = (ref[...].astype(F32) + self.got[1].astype(F32)).astype(BF)
        self.merged_b.start()

    def total(self):
        self.prev_a.wait_recv()
        self.merged_a.wait_recv()
        a = self.chunk(0, 0)[...].astype(F32) + self.got[3].astype(F32) + self.got[4].astype(F32)
        self.next_b.wait_recv()
        self.merged_b.wait_recv()
        b = self.chunk(0, 1)[...].astype(F32) + self.got[2].astype(F32) + self.got[5].astype(F32)
        return a, b

    def drain(self):
        for c in (self.opp_a, self.opp_b, self.next_b, self.prev_a, self.merged_a, self.merged_b):
            c.wait_send()


class RingCopies:
    def __init__(self, own, slot, half, me, ssem, rsem, ahead, behind):
        left, right = lax.rem(me + 3, 4), lax.rem(me + 1, 4)
        far = lax.rem(me + 2, 4)
        self.to_ahead = send(own, slot(me), ssem.at[0], rsem.at[0], ahead)
        self.to_behind = send(own, slot(me), ssem.at[1], rsem.at[1], behind)
        self.on_ahead = send(half(left, 0), half(left, 0), ssem.at[2], rsem.at[2], ahead)
        self.on_behind = send(half(right, 1), half(right, 1), ssem.at[3], rsem.at[3], behind)
        self.from_left = (slot(left), rsem.at[0])
        self.from_right = (slot(right), rsem.at[1])
        self.far_a = (half(far, 0), rsem.at[2])
        self.far_b = (half(far, 1), rsem.at[3])

    def start(self):
        self.to_ahead.start()
        self.to_behind.start()

    def forward(self):
        self.to_ahead.wait_recv()
        self.on_ahead.start()
        self.to_behind.wait_recv()
        self.on_behind.start()

    def finish(self):
        self.on_ahead.wait_recv()
        self.on_behind.wait_recv()

    def drain(self):
        for c in (self.to_ahead, self.to_behind, self.on_ahead, self.on_behind):
            c.wait_send()


def packed_rows(start, count):
    done = 0
    while done < count:
        at = start + done
        take = min(count - done, PIECE - at % PIECE)
        yield done, at // PIECE, at % PIECE, take
        done += take


def normed(values, gain):
    scale = lax.rsqrt(jnp.mean(values * values, axis=-1, keepdims=True) + 1e-06)
    return (values * scale * gain).astype(BF)


def softmax(scores):
    e = jnp.exp(scores - jnp.max(scores, axis=-1, keepdims=True))
    return (e / jnp.sum(e, axis=-1, keepdims=True)).astype(BF)


def attend(queries, keys, values):
    outs = []
    for h in range(queries.shape[1] // HEAD):
        cut = slice(h * HEAD, (h + 1) * HEAD)
        scores = lax.dot_general(
            queries[:, cut], keys[:, cut], (((1,), (1,)), ((), ())), preferred_element_type=F32
        ) * HEAD ** (-0.5)
        outs.append(jnp.dot(softmax(scores), values[:, cut], preferred_element_type=F32).astype(BF))
    return jnp.concatenate(outs, axis=1)


TABLE_ROWS = 4000
STEP = 160
ORDER = (2, 1, 3, 0)


def owner_of(ids):
    return jnp.floor((ids.astype(F32) + 0.5) * (1.0 / TABLE_ROWS)).astype(jnp.int32)


def iota(shape, dim):
    return lax.broadcasted_iota(jnp.int32, shape, dim)


def kernel(
    ids_ref, q_ref, kvp_ref, qkv_ref, so_ref, cq_ref, co_ref, inp_ref, ns_ref, nc_ref, table_ref,
    out_ref,
    asks, ids_got, row_ref, rows_got, place, place_smem, table_bf, table_f32, rows_f32, selector,
    pack, wg, full, kv_chunk, kv_got, kv_y, kv_in, span, mate_span,
    chunk, y_got, z_chunk, z_got, sums, back_out, back_in, back_rows,
    w_qk, w_v, w_cq, w_so, w_co,
    local, ids_s, ids_r, row_s, row_r, wz_s, wz_r, wy_s, wy_r, wx_s, wx_r, wc_s, wc_r,
    ky_s, ky_r, kz_s, kz_r, m_s, m_r, y_s, y_r, z_s, z_r, back_s, back_r,
):
    v, b, x, c, y, z = where_am_i()
    greet(v, b)
    rest = lax.rem(v, 8)
    odd = lax.rem(z, 2)
    ahead = (v, lax.rem(y + 1, 4) * 4 + z)
    behind = (v, lax.rem(y + 3, 4) * 4 + z)
    z_ahead = (v, y * 4 + lax.rem(z + 1, 4))
    z_behind = (v, y * 4 + lax.rem(z + 3, 4))
    z_outside = (v, y * 4 + lax.rem(z + 3 + 2 * odd, 4))
    z_mate = (v, y * 4 + z + 1 - 2 * odd)
    x_ahead = (lax.rem(x + 1, 4) * 8 + rest, b)
    x_behind = (lax.rem(x + 3, 4) * 8 + rest, b)
    mate = (v + 1 - 2 * c, b)

    load_table = pltpu.make_async_copy(table_ref, table_bf, local.at[0])
    load_table.start()

    ids_row = jnp.broadcast_to(ids_ref[...], (128, 128))
    ids_col = ids_row.T
    own_row, own_col = owner_of(ids_row), owner_of(ids_col)
    same = own_row == own_col
    up, across = iota((128, 128), 0), iota((128, 128), 1)
    within_col = jnp.sum(jnp.where(same & (across < up), 1.0, 0.0), axis=1, keepdims=True)
    within_row = jnp.sum(jnp.where(same & (up < across), 1.0, 0.0), axis=0, keepdims=True)
    slot = own_col * 4 + within_col.astype(jnp.int32)
    selector[...] = jnp.where(slot == across, 1.0, 0.0).astype(BF)
    mine = iota((NV, 128), 0) == own_row[:NV]
    lane = iota((NV, 128), 1)
    question = jnp.zeros((NV, 128), jnp.int32)
    for j in range(4):
        hit = mine & (within_row == float(j))
        column = jnp.sum(jnp.where(hit, ids_row[:NV] + 1, 0), axis=1, keepdims=True)
        question = jnp.where(lane == 4 * v + j, column, question)
    asks[...] = question.reshape(NV, 1, 128)

    all_here()

    def ask(o, _):
        to = lax.rem(v + o, NV)
        send(asks.at[to], ids_got.at[v], ids_s.at[o], ids_r.at[o], (to, b)).start()
        return 0

    lax.fori_loop(1, NV, ask, 0)

    ky = RingSum(lambda r, h: kv_chunk.at[r, h], kv_got, ky_s, ky_r, ahead, behind)

    def open_ring(ring, r):
        if r == 2:
            ring.opp_a.start()
            ring.opp_b.start()
        elif r == 1:
            ring.next_b.start()
        elif r == 3:
            ring.prev_a.start()

    for r in ORDER:
        term = jnp.dot(q_ref[lax.rem(y + r, 4)], kvp_ref[...], preferred_element_type=F32)
        kv_chunk[r] = term.reshape(2, 64, 896).astype(BF)
        open_ring(ky, r)

    def put(block, start):
        for at, piece, row, take in packed_rows(start, block.shape[0]):
            pack[piece, row : row + take, :] = block[at : at + take]

    put(qkv_ref[:, 0:896], QK_AT)
    put(jnp.concatenate([qkv_ref[0:28, 896:1344], qkv_ref[28:56, 896:1344]], axis=1), V_AT)
    put(jnp.concatenate([cq_ref[0:28, :], cq_ref[28:56, :]], axis=1), CQ_AT)
    put(so_ref[...], SO_AT)
    put(co_ref[...], CO_AT)
    pack[7] = jnp.zeros_like(pack[7])
    wg[y, z] = pack[x * 2 + c]

    load_table.wait()

    def widen(i, _):
        at = pl.ds(pl.multiple_of(i * STEP, STEP), STEP)
        table_f32[at, :] = table_bf[at, :].astype(F32)
        return 0

    lax.fori_loop(0, TABLE_ROWS // STEP, widen, 0)

    def asked(o, _):
        send(asks.at[v], ids_got.at[v], ids_s.at[o], ids_r.at[o], (v, b)).wait_recv()
        return 0

    lax.fori_loop(1, NV, asked, 0)
    ids_got[v] = asks[v]
    row_ref[...] = jnp.sum(ids_got[...], axis=0)

    def tell(o, _):
        to = lax.rem(b + o, NB)
        send(row_ref, rows_got.at[b], row_s.at[o], row_r.at[o], (v, to)).start()
        return 0

    lax.fori_loop(1, NB, tell, 0)
    rows_got[b] = row_ref[...]

    wz = RingCopies(
        wg.at[y, z], lambda i: wg.at[y, i], lambda i, h: wg.at[y, i, pl.ds(8 * h, 8 + 8 * h)],
        z, wz_s, wz_r, z_ahead, z_behind,
    )
    wz.start()
    ky.merge_a()
    ky.merge_b()
    a, bb = ky.total()
    kv_y[0] = a.astype(BF)
    kv_y[1] = bb.astype(BF)
    half_pair = z // 2
    kz = send(kv_y.at[1 - half_pair], kv_in, kz_s, kz_r, z_outside)
    kz.start()
    wz.forward()

    def told(o, _):
        send(row_ref, rows_got.at[b], row_s.at[o], row_r.at[o], (v, b)).wait_recv()
        return 0

    lax.fori_loop(1, NB, told, 0)
    place[...] = jnp.clip(rows_got[:, 0, :] - 1 - v * TABLE_ROWS, 0, TABLE_ROWS - 1)
    to_scalars = pltpu.make_async_copy(place, place_smem, local.at[1])
    to_scalars.start()
    to_scalars.wait()

    rings = [
        RingSum(lambda r, h, k=k: chunk.at[k, r, h], y_got.at[k], y_s.at[k], y_r.at[k], ahead, behind)
        for k in range(4)
    ]

    def project(k, r):
        peer = lax.rem(y + r, 4) * 4 + lax.rem(z + ORDER[k], 4)

        def eight(i, _):
            for u in range(8):
                at = place_smem[peer, i * 8 + u]
                rows_f32[pl.ds(pl.multiple_of(i * 8, 8) + u, 1), :] = table_f32[pl.ds(at, 1), :]
            return 0

        lax.fori_loop(0, 16, eight, 0)
        term = jnp.dot(rows_f32[...].astype(BF), inp_ref[...], preferred_element_type=F32)
        chunk[k, r] = term.reshape(2, 64, 896).astype(BF)

    zsum = RingSum(lambda r, h: z_chunk.at[r, h], z_got, z_s, z_r, z_ahead, z_behind)

    def settle(k):
        a, bb = rings[k].total()
        z_chunk[ORDER[k], 0] = a.astype(BF)
        z_chunk[ORDER[k], 1] = bb.astype(BF)

    def merge(k):
        rings[k].merge_a()
        rings[k].merge_b()

    def go(k, *which):
        for r in which:
            project(k, r)
            open_ring(rings[k], r)

    go(0, 2, 1, 3)
    go(1, 2)
    project(0, 0)
    merge(0)
    go(1, 1, 3)
    go(2, 2)
    merge(1)
    project(1, 0)
    settle(0)
    zsum.opp_a.start()
    zsum.opp_b.start()
    go(2, 1, 3)
    wz.finish()
    wy = RingCopies(
        wg.at[y], lambda i: wg.at[i], lambda i, h: wg.at[i, pl.ds(2 * h, 2)], y, wy_s, wy_r,
        ahead, behind,
    )
    wy.start()
    go(3, 2)
    merge(2)
    project(2, 0)
    settle(1)
    zsum.next_b.start()
    go(3, 1, 3)
    merge(3)
    wy.forward()
    project(3, 0)
    settle(2)
    zsum.prev_a.start()
    zsum.merge_a()
    zsum.merge_b()
    kz.wait_recv()
    span[...] = (kv_y[half_pair].astype(F32) + kv_in[...].astype(F32)).astype(BF)
    spans = send(span, mate_span, m_s, m_r, z_mate)
    spans.start()
    settle(3)
    wy.finish()

    wx = RingCopies(
        wg, lambda i: full.at[c, i], lambda i, h: full.at[c, i, pl.ds(2 * h, 2)], x,
        wx_s, wx_r, x_ahead, x_behind,
    )
    wx.start()
    to_mate = []

    def pass_on(i, src, dst):
        copy = send(src, dst, wc_s.at[i], wc_r.at[i], mate)
        copy.start()
        to_mate.append(copy)

    pass_on(0, wg, full.at[c, x])
    full[c, x] = wg[...]
    wx.forward()
    for i, o in ((1, 3), (2, 1)):
        slot_ref = full.at[c, lax.rem(x + o, 4)]
        pass_on(i, slot_ref, slot_ref)
    wx.finish()
    slot_ref = full.at[c, lax.rem(x + 2, 4)]
    pass_on(3, slot_ref, slot_ref)

    for copy in to_mate:
        copy.wait_recv()

    def rows_of(peer, start, count):
        return [
            full[piece % 2, piece // 2, peer // 4, peer % 4, row : row + take, :]
            for _, piece, row, take in packed_rows(start, count)
        ]

    def lay(dst, at, parts, lanes):
        for part in parts:
            dst[at : at + part.shape[0], :] = part[:, lanes]
            at += part.shape[0]

    whole = slice(0, 896)
    for peer in range(NB):
        lay(w_qk, 56 * peer, rows_of(peer, QK_AT, 56), whole)
        for dst, start in ((w_v, V_AT), (w_cq, CQ_AT)):
            parts = rows_of(peer, start, 28)
            lay(dst, 56 * peer, parts, slice(0, 448))
            lay(dst, 56 * peer + 28, parts, slice(448, 896))
        lay(w_so, 28 * peer, rows_of(peer, SO_AT, 28), whole)
        lay(w_co, 28 * peer, rows_of(peer, CO_AT, 28), whole)

    a, bb = zsum.total()
    sums[0:64] = a
    sums[64:128] = bb
    for i in range(NV):
        back_out[i] = sums[4 * i : 4 * i + 4, :].astype(BF)

    def give(o, _):
        to = lax.rem(v + o, NV)
        send(back_out.at[to], back_in.at[v], back_s.at[o], back_r.at[o], (to, b)).start()
        return 0

    lax.fori_loop(1, NV, give, 0)
    back_in[v] = back_out[v]

    def given(o, _):
        send(back_out.at[v], back_in.at[v], back_s.at[o], back_r.at[o], (v, b)).wait_recv()
        return 0

    lax.fori_loop(1, NV, given, 0)
    for i in range(NV):
        back_rows[4 * i : 4 * i + 4, :] = back_in[i].astype(F32)
    start = jnp.dot(selector[...], back_rows[...].astype(BF), preferred_element_type=F32)
    stream = start.astype(BF).astype(F32)

    self_in = normed(stream, ns_ref[...])
    qk = jnp.dot(self_in, w_qk[...], preferred_element_type=F32).astype(BF)
    vals = jnp.dot(self_in, w_v[...], preferred_element_type=F32).astype(BF)
    heads = attend(qk[:, 0:448], qk[:, 448:896], vals)
    stream = stream + jnp.dot(heads, w_so[...], preferred_element_type=F32)
    cross_in = normed(stream, nc_ref[...])
    cross_q = jnp.dot(cross_in, w_cq[...], preferred_element_type=F32).astype(BF)
    spans.wait_recv()
    span_kv = (span[...].astype(F32) + mate_span[...].astype(F32)).astype(BF)
    heads = attend(cross_q, span_kv[:, 0:448], span_kv[:, 448:896])
    stream = stream + jnp.dot(heads, w_co[...], preferred_element_type=F32)
    out_ref[...] = stream.astype(BF)

    def sent(count, src, dst, ssem, rsem):
        def one(o, _):
            send(src, dst, ssem.at[o], rsem.at[o], (v, b)).wait_send()
            return 0

        lax.fori_loop(1, count, one, 0)

    sent(NV, asks.at[v], ids_got.at[v], ids_s, ids_r)
    sent(NB, row_ref, rows_got.at[b], row_s, row_r)
    sent(NV, back_out.at[v], back_in.at[v], back_s, back_r)
    for ring in (ky, *rings, zsum, wz, wy, wx):
        ring.drain()
    for copy in (*to_mate, kz, spans):
        copy.wait_send()


DMA = pltpu.SemaphoreType.DMA


def body(
    neighbour_ids, query_states, table, in_proj, kv_proj, norm_self, self_qkv, self_out,
    norm_cross, cross_q, cross_out,
):
    vm = pltpu.VMEM
    out = pl.pallas_call(
        kernel,
        out_shape=jax.ShapeDtypeStruct((128, 896), BF),
        in_specs=[pl.BlockSpec(memory_space=vm)] * 10 + [pl.BlockSpec(memory_space=pl.ANY)],
        out_specs=pl.BlockSpec(memory_space=vm),
        scratch_shapes=[
            vm((NV, 1, 128), jnp.int32), vm((NV, 1, 128), jnp.int32), vm((1, 128), jnp.int32),
            vm((NB, 1, 128), jnp.int32), vm((NB, 128), jnp.int32), pltpu.SMEM((NB, 128), jnp.int32),
            vm((TABLE_ROWS, 256), BF), vm((TABLE_ROWS, 256), F32), vm((128, 256), F32),
            vm((128, 128), BF),
            vm((8, PIECE, 896), BF), vm((4, 4, PIECE, 896), BF), vm((2, 4, 4, 4, PIECE, 896), BF),
            vm((4, 2, 64, 896), BF), vm((6, 64, 896), BF), vm((2, 64, 896), BF),
            vm((64, 896), BF), vm((64, 896), BF), vm((64, 896), BF),
            vm((4, 4, 2, 64, 896), BF), vm((4, 6, 64, 896), BF), vm((4, 2, 64, 896), BF),
            vm((6, 64, 896), BF), vm((128, 896), F32), vm((NV, 4, 896), BF), vm((NV, 4, 896), BF),
            vm((128, 896), F32),
            vm((896, 896), BF), vm((896, 448), BF), vm((896, 448), BF), vm((448, 896), BF),
            vm((448, 896), BF),
            DMA((2,)), DMA((NV,)), DMA((NV,)), DMA((NB,)), DMA((NB,)),
            DMA((4,)), DMA((4,)), DMA((4,)), DMA((4,)), DMA((4,)), DMA((4,)), DMA((4,)), DMA((4,)),
            DMA((6,)), DMA((6,)), DMA, DMA, DMA, DMA, DMA((4, 6)), DMA((4, 6)),
            DMA((6,)), DMA((6,)), DMA((NV,)), DMA((NV,)),
        ],
        compiler_params=pltpu.CompilerParams(
            collective_id=0, has_side_effects=True, vmem_limit_bytes=VMEM_LIMIT
        ),
        name="encoder",
    )(
        neighbour_ids, query_states.reshape(4, 128, 256), kv_proj, self_qkv, self_out, cross_q,
        cross_out, in_proj, norm_self.reshape(1, 896), norm_cross.reshape(1, 896), table,
    )
    return out.reshape(1, 128, 896)


def solution(mesh):
    both = ("vocab", "batch")
    in_specs = (
        P(both, None), P("vocab", None, "batch"), P("vocab", "batch"), P("batch", None),
        P("batch", None), P(), P("batch", None), P("batch", None), P(), P("batch", None),
        P("batch", None),
    )
    return jax.shard_map(
        body, mesh=mesh, in_specs=in_specs, out_specs=P(both, None, None), check_vma=False
    )
```

time: 140 us -> 115 us (0.82)
  Pallas kernels: 123 us -> 110 us
  local copies, waits for them, and re-layouts: 10.4 us -> 4.19 us
  other arithmetic: 6.04 us -> 0 us
    pallas_call x2 -> x1, Pallas kernels: 123 us -> 110 us  [body(): pl.pallas_call(kernel, out_shape=jax.ShapeDtypeStruct((128, 896), BF), in...]
    gather x1 -> x0, local copies, waits for them, and re-layouts: 7.5 us -> none  [body(): looked = jnp.take(table, rows, axis=0)]
    select_n x2 -> x0, other arithmetic: 2.04 us -> none  [the longest x1 1.22 us: body(): looked = jnp.take(table, rows, axis=0)]
    reduce_sum x2 -> x0, other arithmetic: 1.82 us -> none  [the longest x1 1.65 us: body(): asks = jnp.sum(jnp.where(mine & here, ids[:, None, None] + 1, 0), axis=0)]
    eq x3 -> x0, other arithmetic: 1.47 us -> none  [the longest x1 0.72 us: body(): here = ((4 * me + within)[:, None] == lanes[None, :])[:, None, :]]
where the time goes in v2:
time: 115 us; the launch traced here: 114 us
  Pallas kernels  110 us (96%)
  local copies, waits for them, and re-layouts  4.19 us (4%)
    pallas_call x1, Pallas kernels, body(): pl.pallas_call(kernel, out_shape=jax.ShapeDtypeStruct((128, 896), BF), in...  110 us

profile of v2, /device:TPU:1, one launch (start us, length us, event | category | flops | bytes accessed | tf_op | source)
XLA Modules:
  0.0 114.3 jit_solution(10786664964971219142)
XLA Ops:
  0.0 1.3 %reshape.13.ns_ref = f32[1,896]{1,0:T(1,128)} reshape(f32[896]{0:T(1024)} %param.16) | data formatting | bytes 7168 | tf_op jit(solution)/shard_map/reshape | solution.py:512
  1.3 1.3 %reshape.14.nc_ref = f32[1,896]{1,0:T(1,128)} reshape(f32[896]{0:T(1024)} %param.19) | data formatting | bytes 7168 | tf_op jit(solution)/shard_map/reshape | solution.py:512
  2.5 110.1 %encoder.1 = bf16[128,896]{1,0:T(8,128)(2,1)} custom-call(s32[1,128]{1,0:T(1,128)} %ids_ref.1, bf16[4,128,256]{2,1,0:T(8,128)(2,1)} %bitcast.3, bf16[256,896]{1,0:T(8,128)(2,1)} %kvp_ref.1, bf16[56,1344]{1,0:T(8,128)(2,1)} %qkv_ref.1, bf16[28,896]{1,0:T(8,128)(2,1)} %so_ref.1, bf16[56,448]{1,0:T(8,128)(2,1)} %cq_ref.1, bf16[28,896]{1,0:T(8,128)(2,1)} %co_ref.1, ...), custom_call_target="tpu_custom_call" | custom-call | tf_op jit(solution)/shard_map/encoder/pallas_call | solution.py:483
  112.6 1.6 %copy.13 = bf16[1,128,896]{2,1,0:T(8,128)(2,1)} copy(bf16[1,128,896]{2,1,0:T(8,128)(2,1)} %bitcast.2) | data formatting | bytes 458752

commit v3 on v2

--- a/solution.py
+++ b/solution.py
@@ -159,6 +159,7 @@
 TABLE_ROWS = 4000
 STEP = 160
 ORDER = (2, 1, 3, 0)
+GROUPS = ((2, 2), (3, 1), (1, 3), (0, 0))
 
 
 def owner_of(ids):
@@ -170,14 +171,15 @@
 
 
 def kernel(
-    ids_ref, q_ref, kvp_ref, qkv_ref, so_ref, cq_ref, co_ref, inp_ref, ns_ref, nc_ref, table_ref,
+    ids_ref, ns_ref, nc_ref, q_in, kvp_in, qkv_in, so_in, cq_in, co_in, inp_in, table_ref,
     out_ref,
+    q_ref, kvp_ref, qkv_ref, so_ref, cq_ref, co_ref, inp_ref,
     asks, ids_got, row_ref, rows_got, place, place_smem, table_bf, table_f32, rows_f32, selector,
     pack, wg, full, kv_chunk, kv_got, kv_y, kv_in, span, mate_span,
     chunk, y_got, z_chunk, z_got, sums, back_out, back_in, back_rows,
     w_qk, w_v, w_cq, w_so, w_co,
     local, ids_s, ids_r, row_s, row_r, wz_s, wz_r, wy_s, wy_r, wx_s, wx_r, wc_s, wc_r,
-    ky_s, ky_r, kz_s, kz_r, m_s, m_r, y_s, y_r, z_s, z_r, back_s, back_r,
+    ky_s, ky_r, kz_s, kz_r, m_s, m_r, e_s, e_r, y_s, y_r, z_s, z_r, back_s, back_r,
 ):
     v, b, x, c, y, z = where_am_i()
     greet(v, b)
@@ -193,8 +195,16 @@
     x_behind = (lax.rem(x + 3, 4) * 8 + rest, b)
     mate = (v + 1 - 2 * c, b)
 
-    load_table = pltpu.make_async_copy(table_ref, table_bf, local.at[0])
-    load_table.start()
+    pairs = (
+        (table_ref, table_bf), (None, None), (qkv_in, qkv_ref), (so_in, so_ref), (cq_in, cq_ref),
+        (co_in, co_ref), (q_in, q_ref), (kvp_in, kvp_ref), (inp_in, inp_ref),
+    )
+    loads = [
+        pltpu.make_async_copy(src, dst, local.at[i]) if src is not None else None
+        for i, (src, dst) in enumerate(pairs)
+    ]
+    for i in (2, 3, 4, 5, 6, 7, 0, 8):
+        loads[i].start()
 
     ids_row = jnp.broadcast_to(ids_ref[...], (128, 128))
     ids_col = ids_row.T
@@ -223,6 +233,27 @@
 
     lax.fori_loop(1, NV, ask, 0)
 
+    for i in (2, 3, 4, 5):
+        loads[i].wait()
+
+    def put(block, start):
+        for at, piece, row, take in packed_rows(start, block.shape[0]):
+            pack[piece, row : row + take, :] = block[at : at + take]
+
+    put(qkv_ref[:, 0:896], QK_AT)
+    put(jnp.concatenate([qkv_ref[0:28, 896:1344], qkv_ref[28:56, 896:1344]], axis=1), V_AT)
+    put(jnp.concatenate([cq_ref[0:28, :], cq_ref[28:56, :]], axis=1), CQ_AT)
+    put(so_ref[...], SO_AT)
+    put(co_ref[...], CO_AT)
+    pack[7] = jnp.zeros_like(pack[7])
+    wg[y, z] = pack[x * 2 + c]
+
+    wz = RingCopies(
+        wg.at[y, z], lambda i: wg.at[y, i], lambda i, h: wg.at[y, i, pl.ds(8 * h, 8 + 8 * h)],
+        z, wz_s, wz_r, z_ahead, z_behind,
+    )
+    wz.start()
+
     ky = RingSum(lambda r, h: kv_chunk.at[r, h], kv_got, ky_s, ky_r, ahead, behind)
 
     def open_ring(ring, r):
@@ -234,24 +265,14 @@
         elif r == 3:
             ring.prev_a.start()
 
+    loads[6].wait()
+    loads[7].wait()
     for r in ORDER:
         term = jnp.dot(q_ref[lax.rem(y + r, 4)], kvp_ref[...], preferred_element_type=F32)
         kv_chunk[r] = term.reshape(2, 64, 896).astype(BF)
         open_ring(ky, r)
 
-    def put(block, start):
-        for at, piece, row, take in packed_rows(start, block.shape[0]):
-            pack[piece, row : row + take, :] = block[at : at + take]
-
-    put(qkv_ref[:, 0:896], QK_AT)
-    put(jnp.concatenate([qkv_ref[0:28, 896:1344], qkv_ref[28:56, 896:1344]], axis=1), V_AT)
-    put(jnp.concatenate([cq_ref[0:28, :], cq_ref[28:56, :]], axis=1), CQ_AT)
-    put(so_ref[...], SO_AT)
-    put(co_ref[...], CO_AT)
-    pack[7] = jnp.zeros_like(pack[7])
-    wg[y, z] = pack[x * 2 + c]
-
-    load_table.wait()
+    loads[0].wait()
 
     def widen(i, _):
         at = pl.ds(pl.multiple_of(i * STEP, STEP), STEP)
@@ -276,20 +297,37 @@
     lax.fori_loop(1, NB, tell, 0)
     rows_got[b] = row_ref[...]
 
-    wz = RingCopies(
-        wg.at[y, z], lambda i: wg.at[y, i], lambda i, h: wg.at[y, i, pl.ds(8 * h, 8 + 8 * h)],
-        z, wz_s, wz_r, z_ahead, z_behind,
-    )
-    wz.start()
     ky.merge_a()
     ky.merge_b()
+    wz.forward()
     a, bb = ky.total()
     kv_y[0] = a.astype(BF)
     kv_y[1] = bb.astype(BF)
     half_pair = z // 2
-    kz = send(kv_y.at[1 - half_pair], kv_in, kz_s, kz_r, z_outside)
-    kz.start()
-    wz.forward()
+    part = [pl.ds(0, 32), pl.ds(32, 32)]
+    kz = [
+        send(kv_y.at[1 - half_pair, part[i]], kv_in.at[part[i]], kz_s.at[i], kz_r.at[i], z_outside)
+        for i in range(2)
+    ]
+    kz[0].start()
+    kz[1].start()
+    spans = [
+        send(span.at[part[i]], mate_span.at[part[i]], m_s.at[i], m_r.at[i], z_mate)
+        for i in range(2)
+    ]
+
+    def share_span(i):
+        kz[i].wait_recv()
+        total = kv_y[half_pair, part[i]].astype(F32) + kv_in[part[i]].astype(F32)
+        span[part[i]] = total.astype(BF)
+        spans[i].start()
+
+    wz.finish()
+    wy = RingCopies(
+        wg.at[y], lambda i: wg.at[i], lambda i, h: wg.at[i, pl.ds(2 * h, 2)], y, wy_s, wy_r,
+        ahead, behind,
+    )
+    wy.start()
 
     def told(o, _):
         send(row_ref, rows_got.at[b], row_s.at[o], row_r.at[o], (v, b)).wait_recv()
@@ -300,84 +338,64 @@
     to_scalars = pltpu.make_async_copy(place, place_smem, local.at[1])
     to_scalars.start()
     to_scalars.wait()
+    loads[8].wait()
 
     rings = [
         RingSum(lambda r, h, k=k: chunk.at[k, r, h], y_got.at[k], y_s.at[k], y_r.at[k], ahead, behind)
-        for k in range(4)
+        for k in range(1, 4)
     ]
+    early = [
+        RingSum(
+            lambda r, h, i=i: chunk.at[0, r, h, part[i]], y_got.at[0, :, part[i]], e_s.at[i],
+            e_r.at[i], ahead, behind,
+        )
+        for i in range(2)
+    ]
 
     def project(k, r):
-        peer = lax.rem(y + r, 4) * 4 + lax.rem(z + ORDER[k], 4)
-
-        def eight(i, _):
-            for u in range(8):
-                at = place_smem[peer, i * 8 + u]
-                rows_f32[pl.ds(pl.multiple_of(i * 8, 8) + u, 1), :] = table_f32[pl.ds(at, 1), :]
-            return 0
-
-        lax.fori_loop(0, 16, eight, 0)
+        for h in range(2):
+            peer = lax.rem(y + r, 4) * 4 + lax.rem(z + GROUPS[k][h], 4)
+
+            def eight(i, _, h=h, peer=peer):
+                for u in range(8):
+                    at = place_smem[peer, 64 * h + i * 8 + u]
+                    to = pl.ds(pl.multiple_of(i * 8, 8) + 64 * h + u, 1)
+                    rows_f32[to, :] = table_f32[pl.ds(at, 1), :]
+                return 0
+
+            lax.fori_loop(0, 8, eight, 0)
         term = jnp.dot(rows_f32[...].astype(BF), inp_ref[...], preferred_element_type=F32)
         chunk[k, r] = term.reshape(2, 64, 896).astype(BF)
 
-    zsum = RingSum(lambda r, h: z_chunk.at[r, h], z_got, z_s, z_r, z_ahead, z_behind)
+    zsum = [
+        RingSum(
+            lambda r, h, i=i: z_chunk.at[r, h, part[i]], z_got.at[:, part[i]], z_s.at[i],
+            z_r.at[i], z_ahead, z_behind,
+        )
+        for i in range(2)
+    ]
+
+    def settle_early(i):
+        a, bb = early[i].total()
+        z_chunk[2, 0, part[i]] = a.astype(BF)
+        z_chunk[2, 1, part[i]] = bb.astype(BF)
+        zsum[i].opp_a.start()
+        zsum[i].opp_b.start()
 
     def settle(k):
-        a, bb = rings[k].total()
-        z_chunk[ORDER[k], 0] = a.astype(BF)
-        z_chunk[ORDER[k], 1] = bb.astype(BF)
+        a, bb = rings[k - 1].total()
+        z_chunk[GROUPS[k][0], 0] = a.astype(BF)
+        z_chunk[GROUPS[k][1], 1] = bb.astype(BF)
 
     def merge(k):
-        rings[k].merge_a()
-        rings[k].merge_b()
+        rings[k - 1].merge_a()
+        rings[k - 1].merge_b()
 
     def go(k, *which):
         for r in which:
             project(k, r)
-            open_ring(rings[k], r)
-
-    go(0, 2, 1, 3)
-    go(1, 2)
-    project(0, 0)
-    merge(0)
-    go(1, 1, 3)
-    go(2, 2)
-    merge(1)
-    project(1, 0)
-    settle(0)
-    zsum.opp_a.start()
-    zsum.opp_b.start()
-    go(2, 1, 3)
-    wz.finish()
-    wy = RingCopies(
-        wg.at[y], lambda i: wg.at[i], lambda i, h: wg.at[i, pl.ds(2 * h, 2)], y, wy_s, wy_r,
-        ahead, behind,
-    )
-    wy.start()
-    go(3, 2)
-    merge(2)
-    project(2, 0)
-    settle(1)
-    zsum.next_b.start()
-    go(3, 1, 3)
-    merge(3)
-    wy.forward()
-    project(3, 0)
-    settle(2)
-    zsum.prev_a.start()
-    zsum.merge_a()
-    zsum.merge_b()
-    kz.wait_recv()
-    span[...] = (kv_y[half_pair].astype(F32) + kv_in[...].astype(F32)).astype(BF)
-    spans = send(span, mate_span, m_s, m_r, z_mate)
-    spans.start()
-    settle(3)
-    wy.finish()
-
-    wx = RingCopies(
-        wg, lambda i: full.at[c, i], lambda i, h: full.at[c, i, pl.ds(2 * h, 2)], x,
-        wx_s, wx_r, x_ahead, x_behind,
-    )
-    wx.start()
+            open_ring(rings[k - 1], r)
+
     to_mate = []
 
     def pass_on(i, src, dst):
@@ -385,15 +403,89 @@
         copy.start()
         to_mate.append(copy)
 
+    project(0, 2)
+    open_ring(early[0], 2)
+    project(0, 1)
+    open_ring(early[0], 1)
+    share_span(0)
+    open_ring(early[1], 2)
+    project(0, 3)
+    open_ring(early[0], 3)
+    early[0].merge_a()
+    early[0].merge_b()
+    open_ring(early[1], 1)
+    open_ring(early[1], 3)
+    project(0, 0)
+    early[1].merge_a()
+    early[1].merge_b()
+    go(1, 2)
+    settle_early(0)
+    wy.forward()
+    go(1, 1)
+    settle_early(1)
+    go(1, 3)
+    share_span(1)
+
+    wy.finish()
+    wx = RingCopies(
+        wg, lambda i: full.at[c, i], lambda i, h: full.at[c, i, pl.ds(2 * h, 2)], x,
+        wx_s, wx_r, x_ahead, x_behind,
+    )
+    wx.start()
     pass_on(0, wg, full.at[c, x])
+
+    project(2, 2)
+    merge(1)
+    open_ring(rings[1], 2)
+    go(2, 1, 3)
+    project(1, 0)
+    settle(1)
+    for i in range(2):
+        zsum[i].next_b.start()
+        zsum[i].prev_a.start()
     full[c, x] = wg[...]
+    project(3, 2)
+    merge(2)
+    open_ring(rings[2], 2)
+    go(3, 1, 3)
+    project(2, 0)
+    settle(2)
+    project(3, 0)
+    zsum[0].merge_a()
+    zsum[0].merge_b()
+    merge(3)
+    zsum[1].merge_a()
+    zsum[1].merge_b()
     wx.forward()
     for i, o in ((1, 3), (2, 1)):
         slot_ref = full.at[c, lax.rem(x + o, 4)]
         pass_on(i, slot_ref, slot_ref)
+    settle(3)
     wx.finish()
     slot_ref = full.at[c, lax.rem(x + 2, 4)]
     pass_on(3, slot_ref, slot_ref)
+
+    for i in range(2):
+        a, bb = zsum[i].total()
+        sums[0:32] = a
+        sums[32:64] = bb
+        for h in range(2):
+            for q in range(8):
+                row = 32 * h + 4 * q
+                back_out[16 * h + 8 * i + q] = sums[row : row + 4, :].astype(BF)
+
+        def give(n, _, i=i):
+            to = n + 8 * (n // 8) + 8 * i
+            o = lax.rem(to - v + NV, NV)
+
+            @pl.when(o != 0)
+            def _():
+                send(back_out.at[to], back_in.at[v], back_s.at[o], back_r.at[o], (to, b)).start()
+
+            return 0
+
+        lax.fori_loop(0, 16, give, 0)
+    back_in[v] = back_out[v]
 
     for copy in to_mate:
         copy.wait_recv()
@@ -419,20 +511,6 @@
         lay(w_so, 28 * peer, rows_of(peer, SO_AT, 28), whole)
         lay(w_co, 28 * peer, rows_of(peer, CO_AT, 28), whole)
 
-    a, bb = zsum.total()
-    sums[0:64] = a
-    sums[64:128] = bb
-    for i in range(NV):
-        back_out[i] = sums[4 * i : 4 * i + 4, :].astype(BF)
-
-    def give(o, _):
-        to = lax.rem(v + o, NV)
-        send(back_out.at[to], back_in.at[v], back_s.at[o], back_r.at[o], (to, b)).start()
-        return 0
-
-    lax.fori_loop(1, NV, give, 0)
-    back_in[v] = back_out[v]
-
     def given(o, _):
         send(back_out.at[v], back_in.at[v], back_s.at[o], back_r.at[o], (v, b)).wait_recv()
         return 0
@@ -443,14 +521,15 @@
     start = jnp.dot(selector[...], back_rows[...].astype(BF), preferred_element_type=F32)
     stream = start.astype(BF).astype(F32)
 
-    self_in = normed(stream, ns_ref[...])
+    self_in = normed(stream, ns_ref[...].reshape(1, 896))
     qk = jnp.dot(self_in, w_qk[...], preferred_element_type=F32).astype(BF)
     vals = jnp.dot(self_in, w_v[...], preferred_element_type=F32).astype(BF)
     heads = attend(qk[:, 0:448], qk[:, 448:896], vals)
     stream = stream + jnp.dot(heads, w_so[...], preferred_element_type=F32)
-    cross_in = normed(stream, nc_ref[...])
+    cross_in = normed(stream, nc_ref[...].reshape(1, 896))
     cross_q = jnp.dot(cross_in, w_cq[...], preferred_element_type=F32).astype(BF)
-    spans.wait_recv()
+    spans[0].wait_recv()
+    spans[1].wait_recv()
     span_kv = (span[...].astype(F32) + mate_span[...].astype(F32)).astype(BF)
     heads = attend(cross_q, span_kv[:, 0:448], span_kv[:, 448:896])
     stream = stream + jnp.dot(heads, w_co[...], preferred_element_type=F32)
@@ -466,9 +545,9 @@
     sent(NV, asks.at[v], ids_got.at[v], ids_s, ids_r)
     sent(NB, row_ref, rows_got.at[b], row_s, row_r)
     sent(NV, back_out.at[v], back_in.at[v], back_s, back_r)
-    for ring in (ky, *rings, zsum, wz, wy, wx):
+    for ring in (ky, *early, *rings, *zsum, wz, wy, wx):
         ring.drain()
-    for copy in (*to_mate, kz, spans):
+    for copy in (*to_mate, *kz, *spans):
         copy.wait_send()
 
 
@@ -483,9 +562,11 @@
     out = pl.pallas_call(
         kernel,
         out_shape=jax.ShapeDtypeStruct((128, 896), BF),
-        in_specs=[pl.BlockSpec(memory_space=vm)] * 10 + [pl.BlockSpec(memory_space=pl.ANY)],
+        in_specs=[pl.BlockSpec(memory_space=vm)] * 3 + [pl.BlockSpec(memory_space=pl.ANY)] * 8,
         out_specs=pl.BlockSpec(memory_space=vm),
         scratch_shapes=[
+            vm((4, 128, 256), BF), vm((256, 896), BF), vm((56, 1344), BF), vm((28, 896), BF),
+            vm((56, 448), BF), vm((28, 896), BF), vm((256, 896), BF),
             vm((NV, 1, 128), jnp.int32), vm((NV, 1, 128), jnp.int32), vm((1, 128), jnp.int32),
             vm((NB, 1, 128), jnp.int32), vm((NB, 128), jnp.int32), pltpu.SMEM((NB, 128), jnp.int32),
             vm((TABLE_ROWS, 256), BF), vm((TABLE_ROWS, 256), F32), vm((128, 256), F32),
@@ -494,22 +575,23 @@
             vm((4, 2, 64, 896), BF), vm((6, 64, 896), BF), vm((2, 64, 896), BF),
             vm((64, 896), BF), vm((64, 896), BF), vm((64, 896), BF),
             vm((4, 4, 2, 64, 896), BF), vm((4, 6, 64, 896), BF), vm((4, 2, 64, 896), BF),
-            vm((6, 64, 896), BF), vm((128, 896), F32), vm((NV, 4, 896), BF), vm((NV, 4, 896), BF),
+            vm((6, 64, 896), BF), vm((64, 896), F32), vm((NV, 4, 896), BF), vm((NV, 4, 896), BF),
             vm((128, 896), F32),
             vm((896, 896), BF), vm((896, 448), BF), vm((896, 448), BF), vm((448, 896), BF),
             vm((448, 896), BF),
-            DMA((2,)), DMA((NV,)), DMA((NV,)), DMA((NB,)), DMA((NB,)),
+            DMA((9,)), DMA((NV,)), DMA((NV,)), DMA((NB,)), DMA((NB,)),
             DMA((4,)), DMA((4,)), DMA((4,)), DMA((4,)), DMA((4,)), DMA((4,)), DMA((4,)), DMA((4,)),
-            DMA((6,)), DMA((6,)), DMA, DMA, DMA, DMA, DMA((4, 6)), DMA((4, 6)),
-            DMA((6,)), DMA((6,)), DMA((NV,)), DMA((NV,)),
+            DMA((6,)), DMA((6,)), DMA((2,)), DMA((2,)), DMA((2,)), DMA((2,)),
+            DMA((2, 6)), DMA((2, 6)), DMA((4, 6)), DMA((4, 6)), DMA((2, 6)), DMA((2, 6)),
+            DMA((NV,)), DMA((NV,)),
         ],
         compiler_params=pltpu.CompilerParams(
             collective_id=0, has_side_effects=True, vmem_limit_bytes=VMEM_LIMIT
         ),
         name="encoder",
     )(
-        neighbour_ids, query_states.reshape(4, 128, 256), kv_proj, self_qkv, self_out, cross_q,
-        cross_out, in_proj, norm_self.reshape(1, 896), norm_cross.reshape(1, 896), table,
+        neighbour_ids, norm_self, norm_cross, query_states.reshape(4, 128, 256), kv_proj, self_qkv,
+        self_out, cross_q, cross_out, in_proj, table,
     )
     return out.reshape(1, 128, 896)
 

time: 115 us -> 99 us (0.86)
  Pallas kernels: 110 us -> 97.2 us
  local copies, waits for them, and re-layouts: 4.19 us -> 1.65 us
    pallas_call x1, Pallas kernels: 110 us -> 97.2 us  [body(): pl.pallas_call(kernel, out_shape=jax.ShapeDtypeStruct((128, 896), BF), in...]
    reshape x2 -> x0, local copies, waits for them, and re-layouts: 2.54 us -> none  [the longest x1 1.28 us: body(): norm_cross.reshape(1, 896)]
where the time goes in v3:
time: 99 us; the launch traced here: 98.9 us
  Pallas kernels  97.2 us (98%)
  local copies, waits for them, and re-layouts  1.65 us (2%)
    pallas_call x1, Pallas kernels, body(): pl.pallas_call(kernel, out_shape=jax.ShapeDtypeStruct((128, 896), BF), in...  97.2 us

profile of v3, /device:TPU:1, one launch (start us, length us, event | category | flops | bytes accessed | tf_op | source)
XLA Modules:
  0.0 98.9 jit_solution(2826834131656537200)
XLA Ops:
  0.0 97.2 %encoder.1 = bf16[128,896]{1,0:T(8,128)(2,1)} custom-call(s32[1,128]{1,0:T(1,128)} %ids_ref.1, f32[896]{0:T(1024)} %ns_ref.1, f32[896]{0:T(1024)} %nc_ref.1, bf16[4,128,256]{2,1,0:T(8,128)(2,1)} %bitcast.3, bf16[256,896]{1,0:T(8,128)(2,1)} %kvp_in.1, bf16[56,1344]{1,0:T(8,128)(2,1)} %qkv_in.1, bf16[28,896]{1,0:T(8,128)(2,1)} %so_in.1, ...), custom_call_target="tpu_custom_call" | custom-call | tf_op jit(solution)/shard_map/encoder/pallas_call | solution.py:562
  97.2 1.6 %copy.13 = bf16[1,128,896]{2,1,0:T(8,128)(2,1)} copy(bf16[1,128,896]{2,1,0:T(8,128)(2,1)} %bitcast.2) | data formatting | bytes 458752

commit v4 on v3

--- a/solution.py
+++ b/solution.py
@@ -407,7 +407,6 @@
     open_ring(early[0], 2)
     project(0, 1)
     open_ring(early[0], 1)
-    share_span(0)
     open_ring(early[1], 2)
     project(0, 3)
     open_ring(early[0], 3)
@@ -424,7 +423,7 @@
     go(1, 1)
     settle_early(1)
     go(1, 3)
-    share_span(1)
+    share_span(0)
 
     wy.finish()
     wx = RingCopies(
@@ -443,6 +442,7 @@
     for i in range(2):
         zsum[i].next_b.start()
         zsum[i].prev_a.start()
+    share_span(1)
     full[c, x] = wg[...]
     project(3, 2)
     merge(2)

time: 99 us -> 96.6 us (0.976)
  Pallas kernels: 97.2 us -> 94.8 us
    pallas_call x1, Pallas kernels: 97.2 us -> 94.8 us  [body(): pl.pallas_call(kernel, out_shape=jax.ShapeDtypeStruct((128, 896), BF), in...]
where the time goes in v4:
time: 96.6 us; the launch traced here: 96.4 us
  Pallas kernels  94.8 us (98%)
  local copies, waits for them, and re-layouts  1.65 us (2%)
    pallas_call x1, Pallas kernels, body(): pl.pallas_call(kernel, out_shape=jax.ShapeDtypeStruct((128, 896), BF), in...  94.8 us

profile of v4, /device:TPU:1, one launch (start us, length us, event | category | flops | bytes accessed | tf_op | source)
XLA Modules:
  0.0 96.4 jit_solution(9764753207395357813)
XLA Ops:
  0.0 94.8 %encoder.1 = bf16[128,896]{1,0:T(8,128)(2,1)} custom-call(s32[1,128]{1,0:T(1,128)} %ids_ref.1, f32[896]{0:T(1024)} %ns_ref.1, f32[896]{0:T(1024)} %nc_ref.1, bf16[4,128,256]{2,1,0:T(8,128)(2,1)} %bitcast.3, bf16[256,896]{1,0:T(8,128)(2,1)} %kvp_in.1, bf16[56,1344]{1,0:T(8,128)(2,1)} %qkv_in.1, bf16[28,896]{1,0:T(8,128)(2,1)} %so_in.1, ...), custom_call_target="tpu_custom_call" | custom-call | tf_op jit(solution)/shard_map/encoder/pallas_call | solution.py:562
  94.8 1.6 %copy.13 = bf16[1,128,896]{2,1,0:T(8,128)(2,1)} copy(bf16[1,128,896]{2,1,0:T(8,128)(2,1)} %bitcast.2) | data formatting | bytes 458752

commit v5 on v4

--- a/solution.py
+++ b/solution.py
@@ -233,27 +233,6 @@
 
     lax.fori_loop(1, NV, ask, 0)
 
-    for i in (2, 3, 4, 5):
-        loads[i].wait()
-
-    def put(block, start):
-        for at, piece, row, take in packed_rows(start, block.shape[0]):
-            pack[piece, row : row + take, :] = block[at : at + take]
-
-    put(qkv_ref[:, 0:896], QK_AT)
-    put(jnp.concatenate([qkv_ref[0:28, 896:1344], qkv_ref[28:56, 896:1344]], axis=1), V_AT)
-    put(jnp.concatenate([cq_ref[0:28, :], cq_ref[28:56, :]], axis=1), CQ_AT)
-    put(so_ref[...], SO_AT)
-    put(co_ref[...], CO_AT)
-    pack[7] = jnp.zeros_like(pack[7])
-    wg[y, z] = pack[x * 2 + c]
-
-    wz = RingCopies(
-        wg.at[y, z], lambda i: wg.at[y, i], lambda i, h: wg.at[y, i, pl.ds(8 * h, 8 + 8 * h)],
-        z, wz_s, wz_r, z_ahead, z_behind,
-    )
-    wz.start()
-
     ky = RingSum(lambda r, h: kv_chunk.at[r, h], kv_got, ky_s, ky_r, ahead, behind)
 
     def open_ring(ring, r):
@@ -271,6 +250,27 @@
         term = jnp.dot(q_ref[lax.rem(y + r, 4)], kvp_ref[...], preferred_element_type=F32)
         kv_chunk[r] = term.reshape(2, 64, 896).astype(BF)
         open_ring(ky, r)
+
+    for i in (2, 3, 4, 5):
+        loads[i].wait()
+
+    def put(block, start):
+        for at, piece, row, take in packed_rows(start, block.shape[0]):
+            pack[piece, row : row + take, :] = block[at : at + take]
+
+    put(qkv_ref[:, 0:896], QK_AT)
+    put(jnp.concatenate([qkv_ref[0:28, 896:1344], qkv_ref[28:56, 896:1344]], axis=1), V_AT)
+    put(jnp.concatenate([cq_ref[0:28, :], cq_ref[28:56, :]], axis=1), CQ_AT)
+    put(so_ref[...], SO_AT)
+    put(co_ref[...], CO_AT)
+    pack[7] = jnp.zeros_like(pack[7])
+    wg[y, z] = pack[x * 2 + c]
+
+    wz = RingCopies(
+        wg.at[y, z], lambda i: wg.at[y, i], lambda i, h: wg.at[y, i, pl.ds(8 * h, 8 + 8 * h)],
+        z, wz_s, wz_r, z_ahead, z_behind,
+    )
+    wz.start()
 
     loads[0].wait()
 

time: 96.6 us -> 96.5 us (level)
  no operation moved by 1% of the time
where the time goes in v5:
time: 96.5 us; the launch traced here: 96.3 us
  Pallas kernels  94.6 us (98%)
  local copies, waits for them, and re-layouts  1.65 us (2%)
    pallas_call x1, Pallas kernels, body(): pl.pallas_call(kernel, out_shape=jax.ShapeDtypeStruct((128, 896), BF), in...  94.6 us

profile of v5, /device:TPU:1, one launch (start us, length us, event | category | flops | bytes accessed | tf_op | source)
XLA Modules:
  0.0 96.3 jit_solution(1879727650601436362)
XLA Ops:
  0.0 94.6 %encoder.1 = bf16[128,896]{1,0:T(8,128)(2,1)} custom-call(s32[1,128]{1,0:T(1,128)} %ids_ref.1, f32[896]{0:T(1024)} %ns_ref.1, f32[896]{0:T(1024)} %nc_ref.1, bf16[4,128,256]{2,1,0:T(8,128)(2,1)} %bitcast.3, bf16[256,896]{1,0:T(8,128)(2,1)} %kvp_in.1, bf16[56,1344]{1,0:T(8,128)(2,1)} %qkv_in.1, bf16[28,896]{1,0:T(8,128)(2,1)} %so_in.1, ...), custom_call_target="tpu_custom_call" | custom-call | tf_op jit(solution)/shard_map/encoder/pallas_call | solution.py:562
  94.6 1.6 %copy.13 = bf16[1,128,896]{2,1,0:T(8,128)(2,1)} copy(bf16[1,128,896]{2,1,0:T(8,128)(2,1)} %bitcast.2) | data formatting | bytes 458752
